TPU v7x, 512 devices: a 4x2x32 block of a 4x8x32 slice. The times are simulated.
512 devices in a mesh: groups: 2 (over y), parts: 32 (over z), sub: 4 (over x), pair: 2 (over core).
Axes of the slice: x: 4, y: 2, z: 32, core: 2. Of those that a mesh axis runs over, the one named last changes fastest.
The devices are a block of a 4x8x32 slice.
Arguments:
- spectra: bfloat16 [2048, 128, 128], P(('groups', 'parts', 'pair')), parts along dimension 0, may hold values from -6 to 6
- defocus: bfloat16 [2048], P(('groups', 'parts', 'pair')), parts along dimension 0, may hold values from 0.5 to 2
- classes: int32 [2048, 4], P(('groups', 'parts', 'pair')), parts along dimension 0, may hold values from 0 to 31, all different within a row
- poses: int32 [2048, 4], P(('groups', 'parts', 'pair')), parts along dimension 0, may hold values from 0 to 31
- probs: bfloat16 [2048, 4], P(('groups', 'parts', 'pair')), parts along dimension 0, may hold values from 0.049804688 to 1
- counts: int32 [128], P(('groups', 'parts', 'pair')), parts along dimension 0, may hold values from 1 to 16, as said below
- offsets: int32 [32], replicated, may hold values from 0 to 64
- row_kernel: bfloat16 [32, 256, 64], P(None, 'sub'), may hold values from -0.015625 to 0.046875
- col_kernel: bfloat16 [32, 128, 64], replicated, may hold values from -0.015625 to 0.046875
Outputs:
- averages: float32 [64, 256, 256], P('groups', ('sub', 'pair')), parts along dimension 0
There are 2 independent parts, one for each index of `groups`. A program takes and returns all parts, laid end to end along the dimension named above; an argument that names none is the same for every part. Nothing has to cross between parts.
Inputs may be any that keep to these rules, and one draw needn't show every extreme that they name: Only the first counts slots of a shard hold used particles; some shard uses all 16 slots. The 4 classes of a particle differ.
All inputs are finite; a program needn't handle non-finite values.
Results may differ from a plain program's by a relative error of at most 0.0038.
Values may be sent and summed in bfloat16 or wider, within the bound.
No kernel may reach another device: no remote copies, remote signals or barrier semaphores. Data moves between devices by JAX's collectives and lax.ppermute only.
A program may use at most 64 MiB of HBM per device.

v0:
```python
import math

import jax
import jax.numpy as jnp
from jax import lax
from jax.sharding import PartitionSpec as P

GRID = 512
BOX = 256
IROWS = 128
ICOLS = 64
LROWS = 256
LCOLS = 128
BAND = 64
ITERS = 4


blob_width = 1.5
avg_scale = 8.0
floor_value = 1.0
highest = lax.Precision.HIGHEST


def sum_in_order(parts, axes, order):
    shape = [lax.axis_size(a) for a in axes]
    parts = parts.reshape(*shape, *parts.shape[1:])
    parts = parts.transpose(*order, *range(len(axes), parts.ndim))
    parts = parts.reshape(-1, *parts.shape[len(axes) :])
    for k in order:
        parts = lax.psum_scatter(parts, axes[k], scatter_dimension=0, tiled=True)
    return parts[0]


def split_up(value, dim, length):
    shape = value.shape
    parts = value.reshape(*shape[:dim], length, shape[dim] // length, *shape[dim + 1 :])
    return jnp.moveaxis(parts, dim, 0)


def sum_by_axis(value, axes, order, dim):
    length = lax.axis_size(axes)
    return sum_in_order(split_up(value, dim, length), axes, order)


def from_everyone(value, axis):
    copies = jnp.broadcast_to(value, (lax.axis_size(axis), *value.shape))
    return lax.all_to_all(copies, axis, split_axis=0, concat_axis=0, tiled=True)


def laid_out(parts, dim):
    shape = list(parts.shape[1:])
    shape[dim] *= parts.shape[0]
    return jnp.moveaxis(parts, 0, dim).reshape(shape)


def collect(value, axis, dim):
    parts = from_everyone(value, axis)
    return laid_out(parts, dim)


def ctf_planes(spec_block, defocus_block):
    row_freq = jnp.arange(IROWS, dtype=jnp.float32) - IROWS // 2
    col_freq = jnp.arange(ICOLS, dtype=jnp.float32)
    radius = (row_freq[:, None] ** 2 + col_freq[None, :] ** 2) / (ICOLS * ICOLS)
    phases = 20.0 * math.pi * defocus_block.astype(jnp.float32)[:, None, None] * radius[None] + 0.1
    ctf_value = jnp.sin(phases)
    real_plane = ctf_value * spec_block[:, :, :ICOLS].astype(jnp.float32)
    imag_plane = ctf_value * spec_block[:, :, ICOLS:].astype(jnp.float32)
    return jnp.concatenate([real_plane, imag_plane, ctf_value * ctf_value], axis=2).astype(
        jnp.bfloat16
    )


def window_rows(plane_set, start_set):
    return jax.vmap(lambda row_start: lax.dynamic_slice_in_dim(plane_set, row_start, BAND, 0))(
        start_set
    )


def block_terms(planes, weights, pose_block, offsets, kernel_rows, col_kernel):
    chosen = pose_block[:, :, None] == jnp.arange(offsets.shape[0], dtype=jnp.int32)[None, None, :]
    row_starts = jnp.sum(jnp.where(chosen, offsets[None, None, :], 0), axis=2)
    windows = jax.vmap(window_rows)(planes, row_starts)
    rows_k = jnp.take(kernel_rows, pose_block, axis=0)
    cols_k = jnp.take(col_kernel, pose_block, axis=0)
    mixed_rows = jnp.einsum("nkrb,nkbj->nkrj", rows_k, windows, preferred_element_type=jnp.float32)
    mixed_rows = (mixed_rows * weights[:, :, None, None]).astype(jnp.bfloat16)
    shape_set = mixed_rows.shape
    mixed_rows = mixed_rows.reshape(shape_set[0], shape_set[1], shape_set[2], 3, ICOLS)
    spread = jnp.einsum("nkrpi,nkci->nkrpc", mixed_rows, cols_k, preferred_element_type=jnp.float32)
    return spread.reshape(shape_set[0] * shape_set[1], shape_set[2], 3 * LCOLS)


def per_device(spectra, defocus, classes, poses, probs, counts, offsets, row_kernel, col_kernel):
    spectra_all, defocus_all, probs_all = (spectra, defocus, probs)
    classes_all, poses_all, counts_all = (classes, poses, counts)
    list_starts = jnp.zeros((1,), jnp.int32)
    last_item = jnp.sum(counts_all)
    list_ends = jnp.cumsum(counts_all)
    slot_shift = list_starts - (list_ends - counts_all)
    list_count = list_ends.shape[0]
    total_slots = spectra_all.shape[0]
    per_block = 8

    def add_block(block_index, class_grids):
        position = block_index * per_block + jnp.arange(per_block, dtype=jnp.int32)
        alive_slot = position < last_item
        member = jnp.sum((position[:, None] >= list_ends[None, :]).astype(jnp.int32), axis=1)
        member = jnp.minimum(member, list_count - 1)
        chosen = member[:, None] == jnp.arange(list_count, dtype=jnp.int32)[None, :]
        slot_index = position + jnp.sum(jnp.where(chosen, slot_shift[None, :], 0), axis=1)
        slot_index = jnp.clip(slot_index, 0, total_slots - 1)
        spec_block = jnp.take(spectra_all, slot_index, axis=0)
        defocus_block = jnp.take(defocus_all, slot_index, axis=0)
        prob_block = jnp.take(probs_all, slot_index, axis=0)
        class_block = jnp.take(classes_all, slot_index, axis=0)
        pose_block = jnp.take(poses_all, slot_index, axis=0)
        weights = prob_block.astype(jnp.float32) * alive_slot.astype(jnp.float32)[:, None]
        planes = ctf_planes(spec_block, defocus_block)
        insert_terms = block_terms(planes, weights, pose_block, offsets, row_kernel, col_kernel)
        return class_grids.at[class_block.reshape(-1)].add(insert_terms)

    block_count = (last_item + per_block - 1) // per_block
    empty_grid = jnp.zeros((lax.axis_size("parts"), row_kernel.shape[1], 3 * LCOLS), jnp.float32)
    class_grids = lax.fori_loop(0, block_count, add_block, empty_grid)
    flat_grid = class_grids.reshape(-1, 3 * LCOLS)
    owned_rows = sum_by_axis(flat_grid, ("parts", "pair"), (1, 0), 0)
    group_size = lax.axis_size("sub") * lax.axis_size("pair")
    own_rows = owned_rows.shape[0]
    space_block = GRID // group_size
    crop_block = BOX // group_size
    col_freq = jnp.arange(LCOLS, dtype=jnp.int32)
    all_rows = jnp.arange(LROWS, dtype=jnp.int32) - LROWS // 2
    grid_index = jnp.arange(GRID, dtype=jnp.int32)
    col_factor = jnp.where(col_freq == 0, 1.0, 2.0).astype(jnp.float32)
    distance = jnp.minimum(grid_index, GRID - grid_index).astype(jnp.float32)
    blob_axis = jnp.exp(
        -2.0 * math.pi * math.pi * blob_width * blob_width * distance * distance / (GRID * GRID)
    )
    two_pi = 2.0 * math.pi / GRID
    col_angles = two_pi * (col_freq[:, None] * grid_index[None, :] % GRID).astype(jnp.float32)
    col_cos = (col_factor[:, None] * jnp.cos(col_angles) * blob_axis[None, :]).reshape(
        LCOLS, group_size, 1, space_block
    )
    col_sin = (col_factor[:, None] * jnp.sin(col_angles) * blob_axis[None, :]).reshape(
        LCOLS, group_size, 1, space_block
    )
    inverse_table = jnp.concatenate([col_cos, col_sin], axis=2).reshape(LCOLS, -1)
    row_angles = two_pi * (all_rows[:, None] * grid_index[None, :] % GRID).astype(jnp.float32)
    row_inverse = jnp.stack([jnp.cos(row_angles), -jnp.sin(row_angles)], axis=1) / GRID
    row_forward = jnp.stack([jnp.cos(row_angles), -jnp.sin(row_angles)], axis=0)
    row_forward = row_forward.reshape(2, group_size, own_rows, GRID).transpose(1, 0, 2, 3)
    col_back = jnp.stack([jnp.cos(col_angles).T, jnp.sin(col_angles).T], axis=1) / GRID
    weight_plane = owned_rows[:, 2 * LCOLS :]
    rescale = jnp.ones_like(weight_plane)
    for sweep_index in range(ITERS):
        spread_cols = jnp.dot(weight_plane * rescale, inverse_table, precision=highest)
        spread_cols = spread_cols.reshape(own_rows, group_size, 2, space_block)
        image_field = lax.dot_general(
            lax.all_to_all(spread_cols, ("sub", "pair"), split_axis=1, concat_axis=0, tiled=True)[
                :, 0
            ],
            row_inverse,
            (((0, 1), (0, 1)), ((), ())),
            precision=highest,
        )
        image_field = image_field * blob_axis[None, :]
        moved = lax.dot_general(
            row_forward, image_field, (((3,), (1,)), ((), ())), precision=highest
        )
        returned = lax.all_to_all(moved, ("sub", "pair"), split_axis=0, concat_axis=3, tiled=True)
        products = lax.dot_general(
            returned[0], col_back, (((2,), (0,)), ((), ())), precision=highest
        )
        conv_real = products[0, :, 0] + products[1, :, 1]
        conv_imag = products[1, :, 0] - products[0, :, 1]
        rescale = rescale / jnp.maximum(
            jnp.sqrt(conv_real * conv_real + conv_imag * conv_imag), floor_value
        )
    crop_index = jnp.arange(BOX, dtype=jnp.int32) - BOX // 2
    crop_pos = crop_index % GRID
    correction = jnp.sinc(crop_index.astype(jnp.float32) / GRID) ** 2
    crop_angles = two_pi * (col_freq[:, None] * crop_pos[None, :] % GRID).astype(jnp.float32)
    crop_cos = col_factor[:, None] * jnp.cos(crop_angles) / correction[None, :]
    crop_sin = col_factor[:, None] * jnp.sin(crop_angles) / correction[None, :]

    def arrange(first_plane, second_plane):
        return jnp.stack(
            [
                first_plane.reshape(LCOLS, group_size, crop_block),
                second_plane.reshape(LCOLS, group_size, crop_block),
            ],
            axis=2,
        )

    final_table = jnp.concatenate(
        [arrange(crop_cos, crop_sin), arrange(-crop_sin, crop_cos)], axis=0
    )
    final_table = final_table.reshape(2 * LCOLS, -1)
    data_planes = jnp.concatenate(
        [owned_rows[:, :LCOLS] * rescale, owned_rows[:, LCOLS : 2 * LCOLS] * rescale], axis=1
    )
    spread_crop = jnp.dot(data_planes, final_table, precision=highest).reshape(
        own_rows, group_size, 2, crop_block
    )
    crop_row_angles = two_pi * (all_rows[:, None] * crop_pos[None, :] % GRID).astype(jnp.float32)
    crop_inverse = jnp.stack([jnp.cos(crop_row_angles), -jnp.sin(crop_row_angles)], axis=1)
    crop_inverse = crop_inverse * (avg_scale / GRID) / correction[None, None, :]
    averaged = lax.dot_general(
        lax.all_to_all(spread_crop, ("sub", "pair"), split_axis=1, concat_axis=0, tiled=True)[:, 0],
        crop_inverse,
        (((0, 1), (0, 1)), ((), ())),
        precision=highest,
    )
    return collect(averaged[None], "parts", 0)


def solution(mesh):
    placed = (
        P(("groups", "parts", "pair"), None, None),
        P(("groups", "parts", "pair")),
        P(("groups", "parts", "pair"), None),
        P(("groups", "parts", "pair"), None),
        P(("groups", "parts", "pair"), None),
        P(("groups", "parts", "pair")),
        P(),
        P(None, "sub", None),
        P(),
    )
    return jax.shard_map(
        per_device,
        mesh=mesh,
        in_specs=placed,
        out_specs=P("groups", ("sub", "pair"), None),
        check_vma=False,
    )
```

profile of v0, /device:TPU:33, one launch (start us, length us, event | category | flops | bytes accessed | tf_op | source)
XLA Modules:
  0.0 537.2 jit_solution(1731202869597729555)
XLA Ops:
  9.5 2.1 broadcast_in_dim.165
  11.6 34.7 %while.13 = (s32[]{:T(128)}, f32[32,64,384]{2,1,0:T(8,128)}, s32[]{:T(128)}, s32[16,4]{1,0:T(8,128)S(1)}, s32[16,4]{1,0:T(8,128)S(1)}, /*index=5*/bf16[32,64,64]...) while((s32[]{:T(128)}, f32[32,64,384]{2,1,0:T(8,128)}, ...), condition=%wide.region_3.5_spmd, body=%wide.region_0.4_spmd.sunk | while | flops 154950976 | bytes 37964732 | solution.py:125
  14.8 2.1 multiply_convert_fusion.6
  18.6 3.6 gather_fusion.4
  29.0 4.5 copy.114
  33.5 4.5 reshape.1215
  38.8 7.4 %scatter_fusion = f32[32,64,384]{2,1,0:T(8,128)} fusion(f32[32,64,384]{2,1,0:T(8,128)} %get-tuple-element.402, s32[32]{0:T(128)S(1)} %fusion.229, f32[32,64,384]{2,1,0:T(8,128)S(1)} %reshape.1215), kind=kCustom, calls=%fused_computation.8.clone.1 | custom fusion | flops 786432 | bytes 9437312 | tf_op jit(solution)/shard_map/while/body/scatter-add | solution.py:121
  46.3 3.8 copy.69
  50.2 91.5 %reduce-scatter.3.cloned.1.call-done = f32[32,32,384]{2,1,0:T(8,128)} async-done(((f32[64,32,384]{2,1,0:T(8,128)}), f32[32,32,384]{2,1,0:T(8,128)}) %reduce-scatter.3.cloned.1.call-update) | async-done | bytes 1572880 | tf_op jit(solution)/shard_map/reduce_scatter | solution.py:30
  143.6 2.1 fusion.65
  145.8 112.5 %reduce-scatter.5.cloned.1.call-done = f32[1,32,384]{2,1,0:T(8,128)} async-done(((f32[32,32,384]{2,1,0:T(8,128)}), f32[1,32,384]{2,1,0:T(8,128)}) %reduce-scatter.5.cloned.1.call-update) | async-done | bytes 49168 | tf_op jit(solution)/shard_map/reduce_scatter | solution.py:30
  258.2 2.2 fusion.193
  261.3 26.7 %all-to-all-start = ((f32[8,1,4096]{2,1,0:T(1,128)}), f32[8,1,4096]{2,1,0:T(1,128)S(1)}, u32[]{:S(2)}, u32[]{:S(2)}) async-start(f32[8,1,4096]{2,1,0:T(1,128)} %reshape.1154), calls=%async_computation.2 | async-start | bytes 262144 | tf_op jit(solution)/shard_map/all_to_all | solution.py:160
  288.0 2.1 fusion.62
  290.2 3.1 all-to-all-done
  297.5 4.5 all-to-all-start.1
  303.1 4.1 all-to-all-done.1
  311.2 2.2 fusion.196
  313.6 8.6 %all_to_all.140 = f32[8,1,4096]{2,1,0:T(1,128)S(1)} all-to-all(f32[8,1,4096]{2,1,0:T(1,128)S(1)} %reshape.1158), channel_id=1, replica_groups=mesh['groups'=2,'parts'=32,'sub'=4,'pair'=2] {'sub','pair'}, dimensions={0} | all-to-all | bytes 262144 | tf_op jit(solution)/shard_map/all_to_all | solution.py:160
  325.3 8.6 %all_to_all.141 = f32[8,1,4096]{2,1,0:T(1,128)S(1)} all-to-all(f32[8,1,4096]{2,1,0:T(1,128)S(1)} %reshape.1160), channel_id=1, replica_groups=mesh['groups'=2,'parts'=32,'sub'=4,'pair'=2] {'sub','pair'}, dimensions={0} | all-to-all | bytes 262144 | tf_op jit(solution)/shard_map/all_to_all | solution.py:171
  338.0 2.2 fusion.199
  340.4 8.6 %all_to_all.142 = f32[8,1,4096]{2,1,0:T(1,128)S(1)} all-to-all(f32[8,1,4096]{2,1,0:T(1,128)S(1)} %reshape.1162), channel_id=1, replica_groups=mesh['groups'=2,'parts'=32,'sub'=4,'pair'=2] {'sub','pair'}, dimensions={0} | all-to-all | bytes 262144 | tf_op jit(solution)/shard_map/all_to_all | solution.py:160
  353.4 4.5 all-to-all-start.5
  359.9 3.2 all-to-all-done.5
  366.5 2.2 fusion.202
  369.6 4.1 all-to-all-start.6
  373.8 5.3 all-to-all-done.6
  382.8 4.3 all-to-all-start.7
  387.7 4.7 all-to-all-done.7
  396.3 4.1 all-to-all-start.8
  400.4 4.9 all-to-all-done.8
  407.1 121.8 %all_to_all.143 = f32[32,1,32,256]{3,2,1,0:T(8,128)S(1)} all-to-all(f32[32,1,32,256]{3,2,1,0:T(8,128)S(1)} %broadcast_in_dim.168), channel_id=1, replica_groups=mesh['groups'=2,'parts'=32,'sub'=4,'pair'=2] {'parts'}, dimensions={0} | all-to-all | bytes 2097152 | tf_op jit(solution)/shard_map/all_to_all | solution.py:47
  (149 shorter events, 55.5 us)
Async XLA Ops:
  6.5 5.0 copy-start
  6.5 5.0 copy-start.7
  6.6 135.2 %reduce-scatter.3.cloned.1.call-start = ((), (), s32[]{:S(2)}) async-start(), calls=%async_computation.12 | async-start | bytes 4718592 | tf_op jit(solution)/shard_map/reduce_scatter | solution.py:30
  50.2 208.1 %reduce-scatter.5.cloned.1.call-start = ((), (), s32[]{:S(2)}) async-start(), calls=%async_computation.13 | async-start | bytes 1622016 | tf_op jit(solution)/shard_map/reduce_scatter | solution.py:30
  141.8 119.5 %copy-start.11 = (f32[128]{0:T(128)}, f32[128]{0:T(128)S(1)}, u32[]{:S(2)}) copy-start(f32[128]{0:T(128)S(1)} %compare_select_fusion.10) | copy-start | bytes 1540
  142.4 151.3 %copy-start.8 = (s32[256]{0:T(256)}, s32[256]{0:T(256)S(1)}, u32[]{:S(2)}) copy-start(s32[256]{0:T(256)S(1)} %get-tuple-element.298) | copy-start | bytes 3076
  261.3 31.9 %all-to-all-start = ((f32[8,1,4096]{2,1,0:T(1,128)}), f32[8,1,4096]{2,1,0:T(1,128)S(1)}, u32[]{:S(2)}, u32[]{:S(2)}) async-start(f32[8,1,4096]{2,1,0:T(1,128)} %reshape.1154), calls=%async_computation.2 | async-start | bytes 262144 | tf_op jit(solution)/shard_map/all_to_all | solution.py:160
  290.2 33.1 %copy-start.5 = (f32[512]{0:T(512)}, f32[512]{0:T(512)S(1)}, u32[]{:S(2)}) copy-start(f32[512]{0:T(512)S(1)} %fusion.154) | copy-start | bytes 6148
  297.5 9.7 %all-to-all-start.1 = ((f32[8,1,4096]{2,1,0:T(1,128)}), f32[8,1,4096]{2,1,0:T(1,128)S(1)}, u32[]{:S(2)}, u32[]{:S(2)}) async-start(f32[8,1,4096]{2,1,0:T(1,128)} %reshape.1156), calls=%async_computation.3 | async-start | bytes 262144 | tf_op jit(solution)/shard_map/all_to_all | solution.py:171
  310.6 0.6 copy-start.1
  350.1 7.9 %copy-start.9 = (s32[256]{0:T(256)S(1)}, s32[256]{0:T(256)}, u32[]{:S(2)}) copy-start(s32[256]{0:T(256)} %copy-done.8) | copy-start | bytes 3076
  350.1 7.9 %copy-start.10 = (s32[256]{0:T(256)S(1)}, s32[256]{0:T(256)}, u32[]{:S(2)}) copy-start(s32[256]{0:T(256)} %get-tuple-element.297) | copy-start | bytes 3076
  353.4 9.7 %all-to-all-start.5 = ((f32[8,1,4096]{2,1,0:T(1,128)}), f32[8,1,4096]{2,1,0:T(1,128)S(1)}, u32[]{:S(2)}, u32[]{:S(2)}) async-start(f32[8,1,4096]{2,1,0:T(1,128)} %reshape.1164), calls=%async_computation.7 | async-start | bytes 262144 | tf_op jit(solution)/shard_map/all_to_all | solution.py:171
  364.2 16.0 %copy-start.6 = (f32[512]{0:T(512)S(1)}, f32[512]{0:T(512)}, u32[]{:S(2)}) copy-start(f32[512]{0:T(512)} %copy-done.5) | copy-start | bytes 6148
  368.8 18.3 %copy-start.12 = (f32[128]{0:T(128)S(1)}, f32[128]{0:T(128)}, u32[]{:S(2)}) copy-start(f32[128]{0:T(128)} %copy-done.11) | copy-start | bytes 1540
  369.6 9.5 %all-to-all-start.6 = ((f32[8,1,4096]{2,1,0:T(1,128)}), f32[8,1,4096]{2,1,0:T(1,128)S(1)}, u32[]{:S(2)}, u32[]{:S(2)}) async-start(f32[8,1,4096]{2,1,0:T(1,128)} %reshape.1166), calls=%async_computation.8 | async-start | bytes 262144 | tf_op jit(solution)/shard_map/all_to_all | solution.py:160
  380.2 13.9 %copy-start.4 = (f32[1,32,384]{2,1,0:T(8,128)S(1)}, f32[1,32,384]{2,1,0:T(8,128)}, u32[]{:S(2)}) copy-start(f32[1,32,384]{2,1,0:T(8,128)} %reduce-scatter.5.cloned.1.call-done) | copy-start | bytes 147460
  382.8 23.7 %copy-start.2 = (f32[256,1,256]{2,0,1:T(8,128)S(1)}, f32[256,1,256]{2,0,1:T(8,128)}, u32[]{:S(2)}) copy-start(f32[256,1,256]{2,0,1:T(8,128)} %get-tuple-element.291) | copy-start | bytes 786436
  382.8 23.8 %copy-start.3 = (f32[256,1,256]{2,0,1:T(8,128)S(1)}, f32[256,1,256]{2,0,1:T(8,128)}, u32[]{:S(2)}) copy-start(f32[256,1,256]{2,0,1:T(8,128)} %get-tuple-element.292) | copy-start | bytes 786436
  382.8 9.6 %all-to-all-start.7 = ((f32[8,1,4096]{2,1,0:T(1,128)}), f32[8,1,4096]{2,1,0:T(1,128)S(1)}, u32[]{:S(2)}, u32[]{:S(2)}) async-start(f32[8,1,4096]{2,1,0:T(1,128)} %reshape.1168), calls=%async_computation.9 | async-start | bytes 262144 | tf_op jit(solution)/shard_map/all_to_all | solution.py:171
  396.3 9.0 %all-to-all-start.8 = ((f32[8,1,2048]{2,1,0:T(1,128)}), f32[8,1,2048]{2,1,0:T(1,128)S(1)}, u32[]{:S(2)}, u32[]{:S(2)}) async-start(f32[8,1,2048]{2,1,0:T(1,128)} %reshape.1170), calls=%async_computation.10 | async-start | bytes 131072 | tf_op jit(solution)/shard_map/all_to_all | solution.py:210
Sparse Core Ops, SparseCore 0:
  50.3 91.4 reduce-scatter.2
  144.6 113.6 reduce-scatter.4
where the time goes:
time: 548 us; the launch traced here: 537 us
  waiting for transfers between devices  229 us (42%)
  blocking collectives  148 us (27%)
  starting transfers between devices  48.4 us (9%)
  local copies, waits for them, and re-layouts  45.5 us (8%)
  other arithmetic  29.9 us (5%)
  matrix products  21 us (4%)
  between operations  15.1 us (3%)
    reduce_scatter x2, waiting for transfers between devices, sum_in_order(): parts = lax.psum_scatter(parts, axes[k], scatter_dimension=0, tiled=True)  204 us
    all_to_all x1, blocking collectives, from_everyone(): return lax.all_to_all(copies, axis, split_axis=0, concat_axis=0, tiled=True)  122 us
    all_to_all x2, starting transfers between devices, per_device(): lax.all_to_all(spread_cols, ('sub', 'pair'), split_axis=1, concat_axis=0,...  30.8 us
    all_to_all x2, blocking collectives, per_device(): lax.all_to_all(spread_cols, ('sub', 'pair'), split_axis=1, concat_axis=0,...  17.1 us
    all_to_all x3, starting transfers between devices, per_device(): lax.all_to_all(moved, ('sub', 'pair'), split_axis=0, concat_axis=3, tiled...  13.3 us
    all_to_all x3, waiting for transfers between devices, per_device(): lax.all_to_all(moved, ('sub', 'pair'), split_axis=0, concat_axis=3, tiled...  12 us
  transfers between devices with their start and end apart: 8, of which 8 were waited for; matrix products, arithmetic and copies ran while one was open for 2% of the time, Pallas kernels for 0%

commit v1 on v0

v1 whole, which is shorter than its diff:
```python
import functools
import math

import jax
import jax.numpy as jnp
import numpy as np
from jax import lax
from jax.experimental import pallas as pl
from jax.experimental.pallas import tpu as pltpu
from jax.sharding import PartitionSpec as P

GRID = 512
BOX = 256
IROWS = 128
ICOLS = 64
LROWS = 256
LCOLS = 128
BAND = 64
K_TOP = 4
ITERS = 4
LANES = 128
UNROLL = 4
WEIGHTS, DEFOCUS, CLASSES, POSES, COUNT, CORE = 0, K_TOP, K_TOP + 1, 2 * K_TOP + 1, 3 * K_TOP + 1, 3 * K_TOP + 2

blob_width = 1.5
avg_scale = 8.0
floor_value = 1.0

F32 = jnp.float32
BF16 = jnp.bfloat16
NT = (((1,), (1,)), ((), ()))
NN = (((1,), (0,)), ((), ()))


def sine_terms():
    r = np.cos(np.linspace(0.0, np.pi, 4001)) * 0.5
    r = r[np.abs(r) > 1e-3]
    z = r * r
    powers = np.stack([z**k for k in range(6)], axis=1)
    terms, *_ = np.linalg.lstsq(powers, np.sin(np.pi * r) / r, rcond=None)
    return [float(t) for t in terms]


SINE = sine_terms()


def particle_kernel(own, pack_ref, offsets_ref, spec_ref, rk_ref, ck_ref, *rest):
    grid_in, grid_ref, placed_ref, radius_ref = rest if len(rest) == 4 else (None, *rest)
    n_pose, half = rk_ref.shape[0], rk_ref.shape[1] // 2
    count = pack_ref[COUNT, 0].astype(jnp.int32)
    core = pack_ref[CORE, 0].astype(jnp.int32)
    first_row = pl.multiple_of((core if own else 1 - core) * half, half)

    lane = lax.broadcasted_iota(jnp.int32, (1, LANES), 1)
    low = lane < ICOLS
    row_freq = (lax.broadcasted_iota(jnp.int32, (IROWS, LANES), 0) - IROWS // 2).astype(F32)
    col_freq = (lax.broadcasted_iota(jnp.int32, (IROWS, LANES), 1) & (ICOLS - 1)).astype(F32)
    radius_ref[...] = (row_freq * row_freq + col_freq * col_freq) * (10.0 / (ICOLS * ICOLS))

    def place(b, carry):
        rows = rk_ref[b, pl.ds(first_row, half), :].astype(F32)
        rows = jnp.concatenate([rows, jnp.zeros((half, LANES - BAND), F32)], axis=1)
        placed_ref[b] = pltpu.roll(rows, offsets_ref[b], 1).astype(BF16)
        return carry

    lax.fori_loop(0, n_pose, place, 0)
    if grid_in is None:
        grid_ref[...] = jnp.zeros_like(grid_ref)
    else:
        grid_ref[...] = grid_in[...]

    def step(block, carry):
        sums = []
        for u in range(UNROLL):
            n = block * UNROLL + u
            turns = radius_ref[...] * pack_ref[DEFOCUS, n]
            turns = turns - jnp.floor(turns + 0.5)
            t = 2.0 * turns + 0.1 / math.pi
            k = jnp.floor(t + 0.5)
            r = t - k
            z = r * r
            s = SINE[-1]
            for term in SINE[-2::-1]:
                s = s * z + term
            ctf = s * r * (1.0 - 2.0 * k * k)
            data = (ctf * spec_ref[n].astype(F32)).astype(BF16)
            power = jnp.where(low, ctf * ctf, 0.0).astype(BF16)
            planes = jnp.concatenate([data, power], axis=1)
            poses = [pack_ref[POSES + j, n].astype(jnp.int32) for j in range(K_TOP)]
            rows = jnp.concatenate([placed_ref[b] for b in poses], axis=0)
            mixed = lax.dot_general(rows, planes, NN, preferred_element_type=F32)
            for j in range(K_TOP):
                m = mixed[j * half : (j + 1) * half] * pack_ref[WEIGHTS + j, n]
                pair = m[:, :LANES]
                stacked = jnp.concatenate(
                    [jnp.where(low, pair, 0.0), jnp.where(low, 0.0, pair), m[:, LANES:]], axis=0
                ).astype(BF16)
                cols = ck_ref[poses[j]]
                cols = jnp.concatenate([cols, cols], axis=0)
                spread = lax.dot_general(stacked, cols, NN, preferred_element_type=F32)
                sums.append((pack_ref[CLASSES + j, n].astype(jnp.int32), spread))
        for c, spread in sums:
            grid_ref[c] += spread
        return carry

    lax.fori_loop(0, (count + UNROLL - 1) // UNROLL, step, 0)


def insert_particles(pack, offsets, spectra, row_kernel, col_kernel, n_class, grids=None):
    n_pose, rows, _ = row_kernel.shape
    out = (n_class, 3 * (rows // 2), LCOLS)
    smem = pl.BlockSpec(memory_space=pltpu.SMEM)
    vmem = pl.BlockSpec(memory_space=pltpu.VMEM)
    operands = [pack, offsets, spectra, row_kernel, col_kernel]
    if grids is not None:
        operands.append(grids)
    work = spectra.shape[0] * K_TOP * (rows // 2) * 2
    return pl.pallas_call(
        functools.partial(particle_kernel, grids is None),
        out_shape=jax.ShapeDtypeStruct(out, F32),
        in_specs=[smem, smem] + [vmem] * (len(operands) - 2),
        out_specs=vmem,
        scratch_shapes=[
            pltpu.VMEM((n_pose, rows // 2, LANES), BF16),
            pltpu.VMEM((IROWS, LANES), F32),
        ],
        cost_estimate=pl.CostEstimate(
            flops=work * (IROWS * 2 * LANES + 3 * LANES * LCOLS) * 8,
            bytes_accessed=2 * 4 * math.prod(out),
            transcendentals=0,
        ),
        compiler_params=pltpu.CompilerParams(vmem_limit_bytes=32 * 2**20),
        name="insert_particles",
    )(*operands)


def split_bf16(x):
    hi = x.astype(BF16)
    return hi, (x - hi.astype(F32)).astype(BF16)


def dot3(a, b, dims):
    (ah, al), (bh, bl) = a, b
    dot = functools.partial(lax.dot_general, dimension_numbers=dims, preferred_element_type=F32)
    return dot(ah, bh) + (dot(ah, bl) + dot(al, bh))


@functools.cache
def tables(groups):
    grid = np.arange(GRID)
    distance = np.minimum(grid, GRID - grid).astype(np.float64)
    blob = np.exp(-2.0 * np.pi**2 * blob_width**2 * distance**2 / GRID**2)
    angle = 2.0 * np.pi / GRID
    kernel = np.cos(angle * (grid[:, None] * grid[None, :] % GRID)) @ blob / GRID
    rows = np.arange(LROWS) - LROWS // 2
    cols = np.arange(LCOLS)
    factor = np.where(cols == 0, 1.0, 2.0)
    mix_rows = np.concatenate(
        [kernel[(rows[:, None] - rows[None, :]) % GRID], kernel[(rows[:, None] + rows[None, :]) % GRID]], axis=1
    )
    half = 0.5 * factor[:, None]
    mix_cols = np.concatenate(
        [half * kernel[(cols[:, None] - cols[None, :]) % GRID], half * kernel[(cols[:, None] + cols[None, :]) % GRID]],
        axis=1,
    )
    crop = np.arange(BOX) - BOX // 2
    correction = np.sinc(crop / GRID) ** 2
    row_angle = angle * (rows[:, None] * crop[None, :] % GRID)
    last_rows = np.concatenate([np.cos(row_angle), -np.sin(row_angle)], axis=0)
    last_rows = last_rows * (avg_scale / GRID) / correction[None, :]
    col_angle = angle * (crop[:, None] * cols[None, :] % GRID)
    last_cols = np.stack([np.cos(col_angle), np.sin(col_angle)], axis=0)
    last_cols = last_cols * factor[None, None, :] / correction[None, :, None]
    last_cols = last_cols.reshape(2, groups, BOX // groups, LCOLS).transpose(1, 0, 2, 3)
    last_cols = last_cols.reshape(groups, 2 * (BOX // groups), LCOLS)

    def two(x):
        x = x.astype(np.float32)
        hi = x.astype(jnp.bfloat16)
        lo = (x - hi.astype(np.float32)).astype(jnp.bfloat16)
        return np.stack([hi, lo])

    return two(mix_rows), two(mix_cols), two(last_rows), two(last_cols)


def refine_kernel(planes_ref, mix_rows_ref, mix_cols_ref, last_rows_ref, last_cols_ref, out_ref):
    blocks, third = planes_ref.shape[0], planes_ref.shape[1] // 3

    def plane(p):
        return jnp.concatenate([planes_ref[g, p * third : (p + 1) * third] for g in range(blocks)], axis=0).astype(F32)

    weight = plane(2)
    mix_rows = (mix_rows_ref[0], mix_rows_ref[1])
    mix_cols = (mix_cols_ref[0], mix_cols_ref[1])
    scale = jnp.ones_like(weight)
    for _ in range(ITERS):
        half = dot3(split_bf16(weight * scale), mix_cols, NN)
        half = jnp.concatenate([half[:, :LCOLS], half[:, LCOLS:]], axis=0)
        conv = dot3(mix_rows, split_bf16(half), NN)
        scale = scale / jnp.maximum(jnp.abs(conv), floor_value)
    last_cols = (last_cols_ref[0], last_cols_ref[1])
    real = dot3(last_cols, split_bf16(plane(0) * scale), NT)
    imag = dot3(last_cols, split_bf16(plane(1) * scale), NT)
    n = real.shape[0] // 2
    both = jnp.concatenate([real[:n] - imag[n:], real[n:] + imag[:n]], axis=1)
    out = dot3(split_bf16(both), (last_rows_ref[0], last_rows_ref[1]), NN)
    out_ref[...] = out.astype(out_ref.dtype)


def refine_class(planes, mix_rows, mix_cols, last_rows, last_cols):
    vmem = pl.BlockSpec(memory_space=pltpu.VMEM)
    return pl.pallas_call(
        refine_kernel,
        out_shape=jax.ShapeDtypeStruct((last_cols.shape[1] // 2, BOX), BF16),
        in_specs=[vmem] * 5,
        out_specs=vmem,
        cost_estimate=pl.CostEstimate(flops=2 * 10**9, bytes_accessed=3 * 10**6, transcendentals=0),
        compiler_params=pltpu.CompilerParams(vmem_limit_bytes=32 * 2**20),
        name="refine_class",
    )(planes, mix_rows, mix_cols, last_rows, last_cols)


def shift(value, axis, by):
    n = lax.axis_size(axis)
    return lax.ppermute(value, axis, [(i, (i + by) % n) for i in range(n)])


def sum_at_owner(parts, axis):
    here = lax.all_to_all(parts.astype(BF16), axis, split_axis=0, concat_axis=0, tiled=True)
    return jnp.sum(here.astype(F32), axis=0)


def per_device(spectra, defocus, classes, poses, probs, counts, offsets, row_kernel, col_kernel):
    n_slots = spectra.shape[0]
    n_class = lax.axis_size("parts")
    group = lax.axis_size("sub") * lax.axis_size("pair")
    used = (jnp.arange(n_slots, dtype=jnp.int32) < counts[0]).astype(F32)
    pack = jnp.concatenate(
        [
            probs.T.astype(F32) * used[None],
            defocus.astype(F32)[None],
            classes.T.astype(F32),
            poses.T.astype(F32),
            jnp.broadcast_to(counts.astype(F32)[:, None], (1, n_slots)),
            jnp.broadcast_to(lax.axis_index("pair").astype(F32), (1, n_slots)),
        ],
        axis=0,
    )
    other_pack = shift(pack, "pair", 1)
    other_spectra = shift(spectra, "pair", 1)
    kernels = (row_kernel, jnp.swapaxes(col_kernel, 1, 2))
    grids = insert_particles(pack, offsets, spectra, *kernels, n_class)
    grids = insert_particles(other_pack, offsets, other_spectra, *kernels, n_class, grids)
    own = sum_at_owner(grids, "parts")
    planes = lax.all_gather(own, ("sub", "pair"), axis=0, tiled=False)
    mix_rows, mix_cols, last_rows, last_cols = tables(group)
    mine = lax.dynamic_index_in_dim(jnp.asarray(last_cols), lax.axis_index(("sub", "pair")), 1, keepdims=False)
    average = refine_class(planes, jnp.asarray(mix_rows), jnp.asarray(mix_cols), jnp.asarray(last_rows), mine)
    return lax.all_gather(average, "parts", axis=0, tiled=False).astype(F32)


def solution(mesh):
    shards = ("groups", "parts", "pair")
    placed = (
        P(shards, None, None),
        P(shards),
        P(shards, None),
        P(shards, None),
        P(shards, None),
        P(shards),
        P(),
        P(None, "sub", None),
        P(),
    )
    return jax.shard_map(
        per_device,
        mesh=mesh,
        in_specs=placed,
        out_specs=P("groups", ("sub", "pair"), None),
        check_vma=False,
    )
```

time: 548 us -> 231 us (0.42)
  the two profiles are of different devices: /device:TPU:33 before, /device:TPU:40 now
where the time goes in v1:
time: 231 us; the launch traced here: 230 us
  waiting for transfers between devices  85.8 us (37%)
  blocking collectives  68.1 us (29%)
  starting transfers between devices  51.1 us (22%)
  Pallas kernels  15.6 us (7%)
  local copies, waits for them, and re-layouts  4.68 us (2%)
  other arithmetic  4.24 us (2%)
    all_to_all x1, waiting for transfers between devices, sum_at_owner(): lax.all_to_all(parts.astype(BF16), axis, split_axis=0, concat_axis=0, til...  85.8 us
    all_gather x1, blocking collectives, per_device(): return lax.all_gather(average, 'parts', axis=0, tiled=False).astype(F32)  54.4 us
    all_to_all x1, starting transfers between devices, sum_at_owner(): lax.all_to_all(parts.astype(BF16), axis, split_axis=0, concat_axis=0, til...  46.7 us
    all_gather x1, blocking collectives, per_device(): planes = lax.all_gather(own, ('sub', 'pair'), axis=0, tiled=False)  13.7 us
    pallas_call x2, Pallas kernels, insert_particles(): pl.pallas_call(functools.partial(particle_kernel, grids is None), out_sha...  12.3 us
  transfers between devices with their start and end apart: 3, of which 1 were waited for; matrix products, arithmetic and copies ran while one was open for 1% of the time, Pallas kernels for 3%

profile of v1, /device:TPU:40, one launch (start us, length us, event | category | flops | bytes accessed | tf_op | source)
XLA Modules:
  0.0 230.2 jit_solution(9624513095066195952)
XLA Ops:
  0.0 1.9 collective-permute-start.1
  2.6 0.7 multiply_bitcast_fusion
  3.3 0.7 bitcast_convert_fusion
  3.9 0.7 convert_bitcast_fusion
  4.7 0.1 concatenate.3.pack_ref
  4.8 2.4 %collective-permute-start = (f32[15,16]{1,0:T(8,128)S(1)}, f32[15,16]{1,0:T(8,128)S(1)}, u32[]{:S(2)}, u32[]{:S(2)}) collective-permute-start(f32[15,16]{1,0:T(8,128)S(1)} %concatenate.3.pack_ref), channel_id=1, source_target_pairs={{0,1},{1,0},{2,3},{3,2},{4,5},{5,4},{6,7},{7,6},{8,9},{9,8},{10,11... | collective-permute-start | bytes 2888 | tf_op jit(solution)/shard_map/ppermute | solution.py:225
  7.2 0.0 copy-start
  7.2 1.0 copy-done
  8.3 0.0 copy-start.1
  8.3 1.0 copy-done.1
  9.3 0.0 copy-start.3
  9.3 1.0 copy-done.3
  10.3 0.0 copy-start.5
  10.3 0.7 copy-done.5
  11.0 6.5 %insert_particles.2.rest_0_ = f32[32,96,128]{2,1,0:T(8,128)S(1)} custom-call(f32[15,16]{1,0:T(8,128)S(1)} %concatenate.3.pack_ref, s32[32]{0:T(128)S(1)} %copy-done.5, bf16[16,128,128]{2,1,0:T(8,128)(2,1)S(1)} %copy-done, bf16[32,64,64]{2,1,0:T(8,128)(2,1)S(1)} %copy-done.1, bf16[32,64,128]{2,1,0:T(8,128)(2,1)S(1)} %bitcast.19), custom_call_target="tpu_custom_call" | custom-call | flops 2684354560 | bytes 3145728 | tf_op jit(solution)/shard_map/insert_particles/pallas_call | solution.py:118
  17.5 0.0 collective-permute-done.pack_ref
  17.6 0.0 collective-permute-done.1.spec_ref
  17.6 0.0 copy-done.2
  17.6 0.0 copy-done.4
  17.6 5.7 %insert_particles.3 = f32[32,96,128]{2,1,0:T(8,128)S(1)} custom-call(f32[15,16]{1,0:T(8,128)S(1)} %collective-permute-done.pack_ref, s32[32]{0:T(128)S(1)} %copy-done.5, bf16[16,128,128]{2,1,0:T(8,128)(2,1)S(1)} %collective-permute-done.1.spec_ref, bf16[32,64,64]{2,1,0:T(8,128)(2,1)S(1)} %copy-done.2, bf16[32,64,128]{2,1,0:T(8,128)(2,1)S(1)} %bitcast.20, ...), custom_call_target="tpu_custom_call" | custom-call | flops 2684354560 | bytes 3145728 | tf_op jit(solution)/shard_map/insert_particles/pallas_call | solution.py:118
  23.3 1.0 convert_element_type.47
  24.3 46.7 %all-to-all-start = ((bf16[32,96,128]{2,1,0:T(8,128)(2,1)}), bf16[32,96,128]{2,1,0:T(8,128)(2,1)S(1)}, u32[]{:S(2)}, u32[]{:S(2)}) async-start(bf16[32,96,128]{2,1,0:T(8,128)(2,1)} %convert_element_type.47), calls=%async_computation | async-start | bytes 1572864 | tf_op jit(solution)/shard_map/all_to_all | solution.py:229
  71.0 0.8 dynamic-slice_bitcast_fusion.last_cols_ref
  71.8 85.8 %all-to-all-done = bf16[32,96,128]{2,1,0:T(8,128)(2,1)S(1)} async-done(((bf16[32,96,128]{2,1,0:T(8,128)(2,1)}), bf16[32,96,128]{2,1,0:T(8,128)(2,1)S(1)}, u32[]{:S(2)}, u32[]{:S(2)}) %all-to-all-start) | async-done | bytes 786464 | tf_op jit(solution)/shard_map/all_to_all | solution.py:229
  157.6 0.1 convert_reduce_fusion
  157.7 13.7 %all-gather = f32[768,128]{1,0:T(8,128)S(1)} all-gather(f32[96,128]{1,0:T(8,128)S(1)} %convert_reduce_fusion), channel_id=2, replica_groups=mesh['groups'=2,'parts'=32,'sub'=4,'pair'=2] {'sub','pair'}, dimensions={0}, use_global_device_ids=true | all-gather | bytes 442368 | tf_op jit(solution)/shard_map/all_gather | solution.py:255
  171.4 0.0 copy-done.6
  171.4 0.0 copy-done.7
  171.4 0.0 copy-done.8
  171.4 3.4 %refine_class.1 = bf16[32,256]{1,0:T(8,128)(2,1)S(1)} custom-call(f32[8,96,128]{2,1,0:T(8,128)S(1)} %bitcast.18, bf16[2,256,512]{2,1,0:T(8,128)(2,1)S(1)} %copy-done.6, bf16[2,128,256]{2,1,0:T(8,128)(2,1)S(1)} %copy-done.8, bf16[2,512,256]{2,1,0:T(8,128)(2,1)S(1)} %copy-done.7, bf16[2,64,128]{2,1,0:T(8,128)(2,1)S(1)} %dynamic-slice_bitcast_fusion.last_cols_ref), custom_call_target="tpu_custom_call" | custom-call | flops 2000000000 | bytes 3000000 | tf_op jit(solution)/shard_map/refine_class/pallas_call | solution.py:212
  174.8 54.4 %all-gather.1 = bf16[1024,256]{1,0:T(8,128)(2,1)S(1)} all-gather(bf16[32,256]{1,0:T(8,128)(2,1)S(1)} %refine_class.1), channel_id=3, replica_groups=mesh['groups'=2,'parts'=32,'sub'=4,'pair'=2] {'parts'}, dimensions={0}, use_global_device_ids=true | all-gather | bytes 540672 | tf_op jit(solution)/shard_map/all_gather | solution.py:259
  229.1 1.1 convert.2
  (8 shorter events, 0.0 us)
Async XLA Ops:
  0.0 17.6 %collective-permute-start.1 = (bf16[16,128,128]{2,1,0:T(8,128)(2,1)}, bf16[16,128,128]{2,1,0:T(8,128)(2,1)S(1)}, u32[]{:S(2)}, u32[]{:S(2)}) collective-permute-start(bf16[16,128,128]{2,1,0:T(8,128)(2,1)} %spec_ref.1), channel_id=1, source_target_pairs={{0,1},{1,0},{2,3},{3,2},{4,5},{5,4},{6,7},{7,6},{8,9},{9,8},{10,11... | collective-permute-start | bytes 1572872 | tf_op jit(solution)/shard_map/ppermute | solution.py:225
  4.8 12.8 %collective-permute-start = (f32[15,16]{1,0:T(8,128)S(1)}, f32[15,16]{1,0:T(8,128)S(1)}, u32[]{:S(2)}, u32[]{:S(2)}) collective-permute-start(f32[15,16]{1,0:T(8,128)S(1)} %concatenate.3.pack_ref), channel_id=1, source_target_pairs={{0,1},{1,0},{2,3},{3,2},{4,5},{5,4},{6,7},{7,6},{8,9},{9,8},{10,11... | collective-permute-start | bytes 2888 | tf_op jit(solution)/shard_map/ppermute | solution.py:225
  7.2 1.0 copy-start
  8.3 1.0 copy-start.1
  9.3 1.0 copy-start.3
  10.3 0.7 copy-start.5
  11.0 6.6 %copy-start.2 = (bf16[32,64,64]{2,1,0:T(8,128)(2,1)S(1)}, bf16[32,64,64]{2,1,0:T(8,128)(2,1)}, u32[]{:S(2)}) copy-start(bf16[32,64,64]{2,1,0:T(8,128)(2,1)} %rk_ref.3) | copy-start | bytes 786436
  11.0 6.6 %copy-start.4 = (bf16[32,128,64]{1,2,0:T(8,128)(2,1)S(1)}, bf16[32,128,64]{1,2,0:T(8,128)(2,1)}, u32[]{:S(2)}) copy-start(bf16[32,128,64]{1,2,0:T(8,128)(2,1)} %param.21) | copy-start | bytes 1572868
  24.3 147.1 %copy-start.6 = (bf16[2,256,512]{2,1,0:T(8,128)(2,1)S(1)}, bf16[2,256,512]{2,1,0:T(8,128)(2,1)}, u32[]{:S(2)}) copy-start(bf16[2,256,512]{2,1,0:T(8,128)(2,1)} %constant.27.clone.mix_rows_ref) | copy-start | bytes 1572868
  24.3 147.1 %copy-start.7 = (bf16[2,512,256]{2,1,0:T(8,128)(2,1)S(1)}, bf16[2,512,256]{2,1,0:T(8,128)(2,1)}, u32[]{:S(2)}) copy-start(bf16[2,512,256]{2,1,0:T(8,128)(2,1)} %constant.29.clone.last_rows_ref) | copy-start | bytes 1572868
  24.3 147.1 %copy-start.8 = (bf16[2,128,256]{2,1,0:T(8,128)(2,1)S(1)}, bf16[2,128,256]{2,1,0:T(8,128)(2,1)}, u32[]{:S(2)}) copy-start(bf16[2,128,256]{2,1,0:T(8,128)(2,1)} %constant.28.clone.mix_cols_ref) | copy-start | bytes 393220
  24.3 133.3 %all-to-all-start = ((bf16[32,96,128]{2,1,0:T(8,128)(2,1)}), bf16[32,96,128]{2,1,0:T(8,128)(2,1)S(1)}, u32[]{:S(2)}, u32[]{:S(2)}) async-start(bf16[32,96,128]{2,1,0:T(8,128)(2,1)} %convert_element_type.47), calls=%async_computation | async-start | bytes 1572864 | tf_op jit(solution)/shard_map/all_to_all | solution.py:229

commit v2 on v1

--- a/solution.py
+++ b/solution.py
@@ -20,7 +20,10 @@
 ITERS = 4
 LANES = 128
 UNROLL = 4
-WEIGHTS, DEFOCUS, CLASSES, POSES, COUNT, CORE = 0, K_TOP, K_TOP + 1, 2 * K_TOP + 1, 3 * K_TOP + 1, 3 * K_TOP + 2
+ALL_VMEM = 67043328
+WEIGHTS, DEFOCUS, CLASSES, POSES, COUNT, SMALL = 0, K_TOP, K_TOP + 1, 2 * K_TOP + 1, 3 * K_TOP + 1, 16
+NEAR = 4
+FAR = 8
 
 blob_width = 1.5
 avg_scale = 8.0
@@ -44,36 +47,114 @@
 SINE = sine_terms()
 
 
-def particle_kernel(own, pack_ref, offsets_ref, spec_ref, rk_ref, ck_ref, *rest):
-    grid_in, grid_ref, placed_ref, radius_ref = rest if len(rest) == 4 else (None, *rest)
-    n_pose, half = rk_ref.shape[0], rk_ref.shape[1] // 2
-    count = pack_ref[COUNT, 0].astype(jnp.int32)
-    core = pack_ref[CORE, 0].astype(jnp.int32)
-    first_row = pl.multiple_of((core if own else 1 - core) * half, half)
-
+def start_all(pairs, sems):
+    copies = [pltpu.make_async_copy(source, target, sems.at[i]) for i, (source, target) in enumerate(pairs)]
+    for copy in copies:
+        copy.start()
+    return copies
+
+
+def prepare_kernel(
+    counts_in, probs_in, defocus_in, classes_in, poses_in, spec_in,
+    pages_ref, counts_ref, probs_ref, defocus_ref, classes_ref, poses_ref, small_ref, sems,
+):
+    n_slots = spec_in.shape[0]
+    copies = start_all(
+        [
+            (spec_in, pages_ref.at[pl.ds(0, n_slots)]),
+            (counts_in, counts_ref),
+            (probs_in, probs_ref),
+            (defocus_in, defocus_ref),
+            (classes_in, classes_ref),
+            (poses_in, poses_ref),
+        ],
+        sems,
+    )
+    small_ref[...] = jnp.zeros_like(small_ref)
+    pages_ref[n_slots] = jnp.zeros(pages_ref.shape[1:], BF16)
+    for copy in copies[1:]:
+        copy.wait()
+    used = lax.broadcasted_iota(jnp.int32, (K_TOP, n_slots), 1) < counts_ref[0]
+    small_ref[WEIGHTS : WEIGHTS + K_TOP, :n_slots] = jnp.where(used, probs_ref[...].astype(F32), 0.0)
+    small_ref[DEFOCUS : DEFOCUS + 1, :n_slots] = defocus_ref[...].astype(F32)
+    small_ref[CLASSES : CLASSES + K_TOP, :n_slots] = classes_ref[...].astype(F32)
+    small_ref[POSES : POSES + K_TOP, :n_slots] = poses_ref[...].astype(F32)
+    small_ref[COUNT : COUNT + 1, :] = jnp.full((1, LANES), counts_ref[0], jnp.int32).astype(F32)
+    pages_ref[n_slots, :SMALL] = small_ref[...].astype(BF16)
+    copies[0].wait()
+
+
+def prepare(counts, probs, defocus, classes, poses, spectra):
+    n_slots = spectra.shape[0]
+    return pl.pallas_call(
+        prepare_kernel,
+        out_shape=jax.ShapeDtypeStruct((n_slots + 1, IROWS, LANES), BF16),
+        in_specs=[pl.BlockSpec(memory_space=pl.ANY)] * 6,
+        out_specs=pl.BlockSpec(memory_space=pltpu.VMEM),
+        scratch_shapes=[
+            pltpu.SMEM(counts.shape, jnp.int32),
+            pltpu.VMEM(probs.shape, BF16),
+            pltpu.VMEM(defocus.shape, BF16),
+            pltpu.VMEM(classes.shape, jnp.int32),
+            pltpu.VMEM(poses.shape, jnp.int32),
+            pltpu.VMEM((SMALL, LANES), F32),
+            pltpu.SemaphoreType.DMA((6,)),
+        ],
+        cost_estimate=pl.CostEstimate(flops=10**6, bytes_accessed=2 * 10**6, transcendentals=0),
+        compiler_params=pltpu.CompilerParams(vmem_limit_bytes=ALL_VMEM),
+        name="prepare",
+    )(counts, probs, defocus, classes, poses, spectra)
+
+
+def particle_kernel(
+    spread_over, core_ref, offsets_in, rk_in, ck_in, own_in, other_in,
+    out_ref, offsets_ref, rows_ref, cols_ref, pages_ref, placed_ref, total_ref, radius_ref, small_ref, scalars_ref, sems,
+):
+    n_slots = pages_ref.shape[1] - 1
+    n_pose, half = placed_ref.shape[0], placed_ref.shape[1]
+    first_row = pl.multiple_of(core_ref[0] * half, half)
+    copies = start_all(
+        [
+            (offsets_in, offsets_ref),
+            (rk_in.at[:, pl.ds(first_row, half), :], rows_ref),
+            (own_in, pages_ref.at[0]),
+            (other_in, pages_ref.at[1]),
+            (ck_in, cols_ref),
+        ],
+        sems,
+    )
     lane = lax.broadcasted_iota(jnp.int32, (1, LANES), 1)
     low = lane < ICOLS
     row_freq = (lax.broadcasted_iota(jnp.int32, (IROWS, LANES), 0) - IROWS // 2).astype(F32)
     col_freq = (lax.broadcasted_iota(jnp.int32, (IROWS, LANES), 1) & (ICOLS - 1)).astype(F32)
     radius_ref[...] = (row_freq * row_freq + col_freq * col_freq) * (10.0 / (ICOLS * ICOLS))
-
-    def place(b, carry):
-        rows = rk_ref[b, pl.ds(first_row, half), :].astype(F32)
-        rows = jnp.concatenate([rows, jnp.zeros((half, LANES - BAND), F32)], axis=1)
-        placed_ref[b] = pltpu.roll(rows, offsets_ref[b], 1).astype(BF16)
-        return carry
-
-    lax.fori_loop(0, n_pose, place, 0)
-    if grid_in is None:
-        grid_ref[...] = jnp.zeros_like(grid_ref)
-    else:
-        grid_ref[...] = grid_in[...]
+    total_ref[...] = jnp.zeros_like(total_ref)
+    copies[0].wait()
+    copies[1].wait()
+    for b in range(n_pose):
+        band = rows_ref[b].astype(F32)
+        band = jnp.concatenate([band, jnp.zeros((half, LANES - BAND), F32)], axis=1)
+        placed_ref[b] = pltpu.roll(band, offsets_ref[b], 1).astype(BF16)
+    copies[2].wait()
+    copies[3].wait()
+    small_ref[...] = pages_ref[:, n_slots, :SMALL].astype(F32)
+    scalars = pltpu.make_async_copy(small_ref, scalars_ref, sems.at[5])
+    scalars.start()
+    copies[4].wait()
+    scalars.wait()
+
+    def pick(shard, row, n):
+        return scalars_ref[shard, row, n].astype(jnp.int32)
+
+    blocks = [(pick(shard, COUNT, 0) + UNROLL - 1) // UNROLL for shard in range(2)]
 
     def step(block, carry):
+        shard = (block >= blocks[0]).astype(jnp.int32)
+        first = (block - shard * blocks[0]) * UNROLL
         sums = []
         for u in range(UNROLL):
-            n = block * UNROLL + u
-            turns = radius_ref[...] * pack_ref[DEFOCUS, n]
+            n = first + u
+            turns = radius_ref[...] * scalars_ref[shard, DEFOCUS, n]
             turns = turns - jnp.floor(turns + 0.5)
             t = 2.0 * turns + 0.1 / math.pi
             k = jnp.floor(t + 0.5)
@@ -83,55 +164,61 @@
             for term in SINE[-2::-1]:
                 s = s * z + term
             ctf = s * r * (1.0 - 2.0 * k * k)
-            data = (ctf * spec_ref[n].astype(F32)).astype(BF16)
+            data = (ctf * pages_ref[shard, n].astype(F32)).astype(BF16)
             power = jnp.where(low, ctf * ctf, 0.0).astype(BF16)
             planes = jnp.concatenate([data, power], axis=1)
-            poses = [pack_ref[POSES + j, n].astype(jnp.int32) for j in range(K_TOP)]
+            poses = [pick(shard, POSES + j, n) for j in range(K_TOP)]
             rows = jnp.concatenate([placed_ref[b] for b in poses], axis=0)
             mixed = lax.dot_general(rows, planes, NN, preferred_element_type=F32)
             for j in range(K_TOP):
-                m = mixed[j * half : (j + 1) * half] * pack_ref[WEIGHTS + j, n]
+                m = mixed[j * half : (j + 1) * half] * scalars_ref[shard, WEIGHTS + j, n]
                 pair = m[:, :LANES]
                 stacked = jnp.concatenate(
                     [jnp.where(low, pair, 0.0), jnp.where(low, 0.0, pair), m[:, LANES:]], axis=0
                 ).astype(BF16)
-                cols = ck_ref[poses[j]]
+                cols = cols_ref[poses[j]]
                 cols = jnp.concatenate([cols, cols], axis=0)
                 spread = lax.dot_general(stacked, cols, NN, preferred_element_type=F32)
-                sums.append((pack_ref[CLASSES + j, n].astype(jnp.int32), spread))
+                c = pick(shard, CLASSES + j, n)
+                sums.append(((c % spread_over) * (total_ref.shape[0] // spread_over) + c // spread_over, spread))
         for c, spread in sums:
-            grid_ref[c] += spread
+            total_ref[c] += spread
         return carry
 
-    lax.fori_loop(0, (count + UNROLL - 1) // UNROLL, step, 0)
-
-
-def insert_particles(pack, offsets, spectra, row_kernel, col_kernel, n_class, grids=None):
+    lax.fori_loop(0, blocks[0] + blocks[1], step, 0)
+    out_ref[...] = total_ref[...].astype(out_ref.dtype)
+
+
+def insert_particles(core, offsets, row_kernel, col_kernel, pages, other_pages, n_class, spread_over):
     n_pose, rows, _ = row_kernel.shape
-    out = (n_class, 3 * (rows // 2), LCOLS)
-    smem = pl.BlockSpec(memory_space=pltpu.SMEM)
-    vmem = pl.BlockSpec(memory_space=pltpu.VMEM)
-    operands = [pack, offsets, spectra, row_kernel, col_kernel]
-    if grids is not None:
-        operands.append(grids)
-    work = spectra.shape[0] * K_TOP * (rows // 2) * 2
+    half = rows // 2
+    out = (n_class, 3 * half, LCOLS)
+    work = 2 * (pages.shape[0] - 1) * K_TOP * half * 2
     return pl.pallas_call(
-        functools.partial(particle_kernel, grids is None),
-        out_shape=jax.ShapeDtypeStruct(out, F32),
-        in_specs=[smem, smem] + [vmem] * (len(operands) - 2),
-        out_specs=vmem,
+        functools.partial(particle_kernel, spread_over),
+        out_shape=jax.ShapeDtypeStruct(out, BF16),
+        in_specs=[pl.BlockSpec(memory_space=pltpu.SMEM)] + [pl.BlockSpec(memory_space=pl.ANY)] * 5,
+        out_specs=pl.BlockSpec(memory_space=pltpu.VMEM),
         scratch_shapes=[
-            pltpu.VMEM((n_pose, rows // 2, LANES), BF16),
+            pltpu.SMEM(offsets.shape, jnp.int32),
+            pltpu.VMEM((n_pose, half, BAND), BF16),
+            pltpu.VMEM(col_kernel.shape, BF16),
+            pltpu.VMEM((2, *pages.shape), BF16),
+            pltpu.VMEM((n_pose, half, LANES), BF16),
+            pltpu.VMEM(out, F32),
             pltpu.VMEM((IROWS, LANES), F32),
+            pltpu.VMEM((2, SMALL, LANES), F32),
+            pltpu.SMEM((2, SMALL, LANES), F32),
+            pltpu.SemaphoreType.DMA((6,)),
         ],
         cost_estimate=pl.CostEstimate(
             flops=work * (IROWS * 2 * LANES + 3 * LANES * LCOLS) * 8,
-            bytes_accessed=2 * 4 * math.prod(out),
+            bytes_accessed=2 * 2 * math.prod(out),
             transcendentals=0,
         ),
-        compiler_params=pltpu.CompilerParams(vmem_limit_bytes=32 * 2**20),
+        compiler_params=pltpu.CompilerParams(vmem_limit_bytes=ALL_VMEM),
         name="insert_particles",
-    )(*operands)
+    )(core, offsets, row_kernel, col_kernel, pages, other_pages)
 
 
 def split_bf16(x):
@@ -225,38 +312,51 @@
     return lax.ppermute(value, axis, [(i, (i + by) % n) for i in range(n)])
 
 
+def neighbours(n, size):
+    return [[first + i for i in range(size)] for first in range(0, n, size)]
+
+
+def strided(n, stride):
+    return [list(range(first, n, stride)) for first in range(stride)]
+
+
+def added(parts):
+    total = parts[0].astype(F32)
+    for i in range(1, parts.shape[0]):
+        total = total + parts[i].astype(F32)
+    return total
+
+
 def sum_at_owner(parts, axis):
-    here = lax.all_to_all(parts.astype(BF16), axis, split_axis=0, concat_axis=0, tiled=True)
-    return jnp.sum(here.astype(F32), axis=0)
+    n = lax.axis_size(axis)
+    parts = parts.reshape(NEAR, n // NEAR, *parts.shape[1:])
+    parts = lax.all_to_all(parts, axis, 0, 0, axis_index_groups=neighbours(n, NEAR))
+    parts = added(parts).astype(BF16)
+    parts = lax.all_to_all(parts, axis, 0, 0, axis_index_groups=strided(n, NEAR))
+    return added(parts)
+
+
+def from_all(value, axis):
+    n = lax.axis_size(axis)
+    far = lax.all_gather(value, axis, axis=0, axis_index_groups=strided(n, FAR))
+    every = lax.all_gather(far, axis, axis=0, axis_index_groups=neighbours(n, FAR))
+    return jnp.swapaxes(every, 0, 1).reshape(n, *value.shape)
 
 
 def per_device(spectra, defocus, classes, poses, probs, counts, offsets, row_kernel, col_kernel):
-    n_slots = spectra.shape[0]
     n_class = lax.axis_size("parts")
     group = lax.axis_size("sub") * lax.axis_size("pair")
-    used = (jnp.arange(n_slots, dtype=jnp.int32) < counts[0]).astype(F32)
-    pack = jnp.concatenate(
-        [
-            probs.T.astype(F32) * used[None],
-            defocus.astype(F32)[None],
-            classes.T.astype(F32),
-            poses.T.astype(F32),
-            jnp.broadcast_to(counts.astype(F32)[:, None], (1, n_slots)),
-            jnp.broadcast_to(lax.axis_index("pair").astype(F32), (1, n_slots)),
-        ],
-        axis=0,
-    )
-    other_pack = shift(pack, "pair", 1)
-    other_spectra = shift(spectra, "pair", 1)
-    kernels = (row_kernel, jnp.swapaxes(col_kernel, 1, 2))
-    grids = insert_particles(pack, offsets, spectra, *kernels, n_class)
-    grids = insert_particles(other_pack, offsets, other_spectra, *kernels, n_class, grids)
+    pages = prepare(counts, probs.T, defocus[None], classes.T, poses.T, spectra)
+    other_pages = shift(pages, "pair", 1)
+    core = lax.axis_index("pair").reshape(1)
+    col_rows = jnp.swapaxes(col_kernel, 1, 2)
+    grids = insert_particles(core, offsets, row_kernel, col_rows, pages, other_pages, n_class, NEAR)
     own = sum_at_owner(grids, "parts")
     planes = lax.all_gather(own, ("sub", "pair"), axis=0, tiled=False)
     mix_rows, mix_cols, last_rows, last_cols = tables(group)
     mine = lax.dynamic_index_in_dim(jnp.asarray(last_cols), lax.axis_index(("sub", "pair")), 1, keepdims=False)
     average = refine_class(planes, jnp.asarray(mix_rows), jnp.asarray(mix_cols), jnp.asarray(last_rows), mine)
-    return lax.all_gather(average, "parts", axis=0, tiled=False).astype(F32)
+    return from_all(average, "parts").astype(F32)
 
 
 def solution(mesh):

time: 231 us -> 211 us (0.913)
  waiting for transfers between devices: 85.8 us -> 33.3 us
  blocking collectives: 68.1 us -> 117 us
  starting transfers between devices: 51.1 us -> 42.5 us
  other arithmetic: 4.24 us -> 0.92 us
  local copies, waits for them, and re-layouts: 4.68 us -> 1.85 us
    all_to_all x1, waiting for transfers between devices: 85.8 us -> 31.1 us  [sum_at_owner(): lax.all_to_all(parts, axis, 0, 0, axis_index_groups=strided(n, NEAR))]
    all_to_all x0 -> x1, blocking collectives: none -> 28.4 us  [sum_at_owner(): lax.all_to_all(parts, axis, 0, 0, axis_index_groups=neighbours(n, NEAR))]
    all_gather x1 -> x2, blocking collectives: 54.4 us -> 75 us  [the longest x1 48.1 us: from_all(): lax.all_gather(far, axis, axis=0, axis_index_groups=neighbours(n, FAR))]
    all_to_all x1, starting transfers between devices: 46.7 us -> 40.5 us  [sum_at_owner(): lax.all_to_all(parts, axis, 0, 0, axis_index_groups=strided(n, NEAR))]
    unnamed x18 -> x6, local copies, waits for them, and re-layouts: 3.79 us -> 0.01 us
    convert_element_type x4 -> x1, other arithmetic: 2.78 us -> 0.11 us  [per_device(): return from_all(average, 'parts').astype(F32)]
    ppermute x2 -> x1, starting transfers between devices: 4.37 us -> 1.95 us  [shift(): return lax.ppermute(value, axis, [(i, (i + by) % n) for i in range(n)])]
  transfers between devices with their start and end apart: 3 -> 2, of which waited for: 1 -> 2; matrix products, arithmetic and copies ran while one was open for 1% -> 0% of each run, Pallas kernels for 3% -> 0%
where the time goes in v2:
time: 211 us; the launch traced here: 210 us
  blocking collectives  117 us (55%)
  starting transfers between devices  42.5 us (20%)
  waiting for transfers between devices  33.3 us (16%)
  Pallas kernels  13.4 us (6%)
    all_gather x1, blocking collectives, from_all(): lax.all_gather(far, axis, axis=0, axis_index_groups=neighbours(n, FAR))  48.1 us
    all_to_all x1, starting transfers between devices, sum_at_owner(): lax.all_to_all(parts, axis, 0, 0, axis_index_groups=strided(n, NEAR))  40.5 us
    all_to_all x1, waiting for transfers between devices, sum_at_owner(): lax.all_to_all(parts, axis, 0, 0, axis_index_groups=strided(n, NEAR))  31.1 us
    all_to_all x1, blocking collectives, sum_at_owner(): lax.all_to_all(parts, axis, 0, 0, axis_index_groups=neighbours(n, NEAR))  28.4 us
    all_gather x1, blocking collectives, from_all(): far = lax.all_gather(value, axis, axis=0, axis_index_groups=strided(n, FAR))  26.9 us
    all_gather x1, blocking collectives, per_device(): planes = lax.all_gather(own, ('sub', 'pair'), axis=0, tiled=False)  13.7 us
    pallas_call x1, Pallas kernels, insert_particles(): pl.pallas_call(functools.partial(particle_kernel, spread_over), out_shape...  8.15 us
  transfers between devices with their start and end apart: 2, of which 2 were waited for; matrix products, arithmetic and copies ran while one was open for 0% of the time, Pallas kernels for 0%

profile of v2, /device:TPU:40, one launch (start us, length us, event | category | flops | bytes accessed | tf_op | source)
XLA Modules:
  0.0 209.8 jit_solution(7596381018554580341)
XLA Ops:
  0.7 1.9 prepare.1.own_in
  2.6 2.0 collective-permute-start
  4.5 2.3 %collective-permute-done.other_in = bf16[17,128,128]{2,1,0:T(8,128)(2,1)} collective-permute-done((bf16[17,128,128]{2,1,0:T(8,128)(2,1)}, bf16[17,128,128]{2,1,0:T(8,128)(2,1)}, u32[]{:S(2)}, u32[]{:S(2)}) %collective-permute-start) | collective-permute-done | bytes 557088 | tf_op jit(solution)/shard_map/ppermute | solution.py:312
  6.8 8.1 %insert_particles.1 = bf16[32,96,128]{2,1,0:T(8,128)(2,1)} custom-call(s32[1]{0:T(128)} %bitcast.core_ref, s32[32]{0:T(128)} %offsets_in.1, bf16[32,64,64]{2,1,0:T(8,128)(2,1)} %rk_in.1, bf16[32,64,128]{2,1,0:T(8,128)(2,1)} %bitcast.24, bf16[17,128,128]{2,1,0:T(8,128)(2,1)} %prepare.1.own_in, bf16[17,128,128]{2,1,0:T(8,128)(2,1)} %collective-permute-done.other_in), custom_call_target="tpu_custom_call" | custom-call | flops 5368709120 | bytes 1572864 | tf_op jit(solution)/shard_map/insert_particles/pallas_call | solution.py:197
  14.9 28.4 %all_to_all.10 = bf16[4,8,96,128]{3,2,1,0:T(8,128)(2,1)S(1)} all-to-all(bf16[4,8,96,128]{3,2,1,0:T(8,128)(2,1)} %bitcast.18), channel_id=1, replica_groups={{0,8,16,24},{32,40,48,56},{64,72,80,88},{96,104,112,120},{128,136,144,1..., dimensions={0} | all-to-all | bytes 1572864 | tf_op jit(solution)/shard_map/all_to_all | solution.py:333
  43.3 0.0 copy-start.2
  43.3 0.8 fusion
  44.1 0.0 copy-start
  44.1 0.0 copy-start.1
  44.1 40.5 %all-to-all-start.1 = ((bf16[8,96,128]{2,1,0:T(8,128)(2,1)}), bf16[8,96,128]{2,1,0:T(8,128)(2,1)S(1)}, u32[]{:S(2)}, u32[]{:S(2)}) async-start(bf16[8,96,128]{2,1,0:T(8,128)(2,1)} %fusion), calls=%async_computation.1 | async-start | bytes 393216 | tf_op jit(solution)/shard_map/all_to_all | solution.py:335
  84.6 0.8 dynamic-slice_bitcast_fusion.last_cols_ref
  85.4 31.1 %all-to-all-done.1 = bf16[8,96,128]{2,1,0:T(8,128)(2,1)S(1)} async-done(((bf16[8,96,128]{2,1,0:T(8,128)(2,1)}), bf16[8,96,128]{2,1,0:T(8,128)(2,1)S(1)}, u32[]{:S(2)}, u32[]{:S(2)}) %all-to-all-start.1) | async-done | bytes 196640 | tf_op jit(solution)/shard_map/all_to_all | solution.py:335
  116.5 13.7 %all_gather.16.planes_ref = f32[8,96,128]{2,1,0:T(8,128)S(1)} all-gather(f32[1,96,128]{2,1,0:T(8,128)S(1)} %convert_add_fusion), channel_id=1, replica_groups=mesh['groups'=2,'parts'=32,'sub'=4,'pair'=2] {'sub','pair'}, dimensions={0}, use_global_device_ids=true | all-gather | bytes 442368 | tf_op jit(solution)/shard_map/all_gather | solution.py:355
  130.2 0.0 copy-done.2
  130.2 0.0 copy-done
  130.2 0.0 copy-done.1
  130.2 3.3 %refine_class.1 = bf16[32,256]{1,0:T(8,128)(2,1)S(1)} custom-call(f32[8,96,128]{2,1,0:T(8,128)S(1)} %all_gather.16.planes_ref, bf16[2,256,512]{2,1,0:T(8,128)(2,1)S(1)} %copy-done.1, bf16[2,128,256]{2,1,0:T(8,128)(2,1)S(1)} %copy-done.2, bf16[2,512,256]{2,1,0:T(8,128)(2,1)S(1)} %copy-done, bf16[2,64,128]{2,1,0:T(8,128)(2,1)S(1)} %dynamic-slice_bitcast_fusion.last_cols_ref), custom_call_target="tpu_custom_call" | custom-call | flops 2000000000 | bytes 3000000 | tf_op jit(solution)/shard_map/refine_class/pallas_call | solution.py:299
  133.6 26.9 %all-gather = bf16[128,256]{1,0:T(8,128)(2,1)S(1)} all-gather(bf16[32,256]{1,0:T(8,128)(2,1)S(1)} %refine_class.1), channel_id=2, replica_groups={{0,64,128,192},{8,72,136,200},{16,80,144,208},{24,88,152,216},{32,96,16..., dimensions={0}, use_global_device_ids=true | all-gather | bytes 81920 | tf_op jit(solution)/shard_map/all_gather | solution.py:341
  160.5 48.1 %all-gather.1 = bf16[32,32,256]{2,1,0:T(8,128)(2,1)S(1)} all-gather(bf16[4,32,256]{2,1,0:T(8,128)(2,1)S(1)} %bitcast.19), channel_id=3, replica_groups={{0,8,16,24,32,40,48,56},{64,72,80,88,96,104,112,120},{128,136,144,152,1..., dimensions={0}, use_global_device_ids=true | all-gather | bytes 589824 | tf_op jit(solution)/shard_map/all_gather | solution.py:342
  208.6 0.1 convert_bitcast_fusion
  208.7 1.1 copy.15
  (1 shorter events, 0.0 us)
Async XLA Ops:
  2.6 4.2 %collective-permute-start = (bf16[17,128,128]{2,1,0:T(8,128)(2,1)}, bf16[17,128,128]{2,1,0:T(8,128)(2,1)}, u32[]{:S(2)}, u32[]{:S(2)}) collective-permute-start(bf16[17,128,128]{2,1,0:T(8,128)(2,1)} %prepare.1.own_in), channel_id=1, source_target_pairs={{0,1},{1,0},{2,3},{3,2},{4,5},{5,4},{6,7},{7,6},{8,9},{9,8},{10,11... | collective-permute-start | bytes 1671176 | tf_op jit(solution)/shard_map/ppermute | solution.py:312
  43.3 86.9 %copy-start.2 = (bf16[2,128,256]{2,1,0:T(8,128)(2,1)S(1)}, bf16[2,128,256]{2,1,0:T(8,128)(2,1)}, u32[]{:S(2)}) copy-start(bf16[2,128,256]{2,1,0:T(8,128)(2,1)} %constant.26.clone.mix_cols_ref) | copy-start | bytes 393220
  44.1 86.1 %copy-start = (bf16[2,512,256]{2,1,0:T(8,128)(2,1)S(1)}, bf16[2,512,256]{2,1,0:T(8,128)(2,1)}, u32[]{:S(2)}) copy-start(bf16[2,512,256]{2,1,0:T(8,128)(2,1)} %constant.27.clone.last_rows_ref) | copy-start | bytes 1572868
  44.1 86.1 %copy-start.1 = (bf16[2,256,512]{2,1,0:T(8,128)(2,1)S(1)}, bf16[2,256,512]{2,1,0:T(8,128)(2,1)}, u32[]{:S(2)}) copy-start(bf16[2,256,512]{2,1,0:T(8,128)(2,1)} %constant.25.clone.mix_rows_ref) | copy-start | bytes 1572868
  44.1 72.4 %all-to-all-start.1 = ((bf16[8,96,128]{2,1,0:T(8,128)(2,1)}), bf16[8,96,128]{2,1,0:T(8,128)(2,1)S(1)}, u32[]{:S(2)}, u32[]{:S(2)}) async-start(bf16[8,96,128]{2,1,0:T(8,128)(2,1)} %fusion), calls=%async_computation.1 | async-start | bytes 393216 | tf_op jit(solution)/shard_map/all_to_all | solution.py:335

commit v3 on v2

--- a/solution.py
+++ b/solution.py
@@ -23,7 +23,6 @@
 ALL_VMEM = 67043328
 WEIGHTS, DEFOCUS, CLASSES, POSES, COUNT, SMALL = 0, K_TOP, K_TOP + 1, 2 * K_TOP + 1, 3 * K_TOP + 1, 16
 NEAR = 4
-FAR = 8
 
 blob_width = 1.5
 avg_scale = 8.0
@@ -107,19 +106,24 @@
 
 
 def particle_kernel(
-    spread_over, core_ref, offsets_in, rk_in, ck_in, own_in, other_in,
-    out_ref, offsets_ref, rows_ref, cols_ref, pages_ref, placed_ref, total_ref, radius_ref, small_ref, scalars_ref, sems,
+    place_ref, offsets_in, rk_in, ck_in, own_in, other_in,
+    out0_ref, out1_ref, out2_ref, out3_ref,
+    offsets_ref, rows_ref, cols_ref, pages_ref, placed_ref, total_ref, radius_ref, page_ref, small_ref, scalars_ref, sems,
 ):
-    n_slots = pages_ref.shape[1] - 1
+    n_slots = pages_ref.shape[1]
+    n_class = total_ref.shape[0]
     n_pose, half = placed_ref.shape[0], placed_ref.shape[1]
-    first_row = pl.multiple_of(core_ref[0] * half, half)
+    first_row = pl.multiple_of(place_ref[0] * half, half)
+    up = NEAR - place_ref[1]
     copies = start_all(
         [
+            (own_in.at[n_slots, pl.ds(0, SMALL)], page_ref.at[0]),
+            (other_in.at[n_slots, pl.ds(0, SMALL)], page_ref.at[1]),
             (offsets_in, offsets_ref),
             (rk_in.at[:, pl.ds(first_row, half), :], rows_ref),
-            (own_in, pages_ref.at[0]),
-            (other_in, pages_ref.at[1]),
+            (own_in.at[pl.ds(0, n_slots)], pages_ref.at[0]),
             (ck_in, cols_ref),
+            (other_in.at[pl.ds(0, n_slots)], pages_ref.at[1]),
         ],
         sems,
     )
@@ -131,17 +135,18 @@
     total_ref[...] = jnp.zeros_like(total_ref)
     copies[0].wait()
     copies[1].wait()
+    small_ref[...] = page_ref[...].astype(F32)
+    scalars = pltpu.make_async_copy(small_ref, scalars_ref, sems.at[7])
+    scalars.start()
+    copies[2].wait()
+    copies[3].wait()
     for b in range(n_pose):
         band = rows_ref[b].astype(F32)
         band = jnp.concatenate([band, jnp.zeros((half, LANES - BAND), F32)], axis=1)
         placed_ref[b] = pltpu.roll(band, offsets_ref[b], 1).astype(BF16)
-    copies[2].wait()
-    copies[3].wait()
-    small_ref[...] = pages_ref[:, n_slots, :SMALL].astype(F32)
-    scalars = pltpu.make_async_copy(small_ref, scalars_ref, sems.at[5])
-    scalars.start()
-    copies[4].wait()
     scalars.wait()
+    for copy in copies[4:]:
+        copy.wait()
 
     def pick(shard, row, n):
         return scalars_ref[shard, row, n].astype(jnp.int32)
@@ -180,36 +185,38 @@
                 cols = jnp.concatenate([cols, cols], axis=0)
                 spread = lax.dot_general(stacked, cols, NN, preferred_element_type=F32)
                 c = pick(shard, CLASSES + j, n)
-                sums.append(((c % spread_over) * (total_ref.shape[0] // spread_over) + c // spread_over, spread))
+                sums.append((((c + up) % NEAR) * (n_class // NEAR) + c // NEAR, spread))
         for c, spread in sums:
             total_ref[c] += spread
         return carry
 
     lax.fori_loop(0, blocks[0] + blocks[1], step, 0)
-    out_ref[...] = total_ref[...].astype(out_ref.dtype)
-
-
-def insert_particles(core, offsets, row_kernel, col_kernel, pages, other_pages, n_class, spread_over):
+    for d, out_ref in enumerate((out0_ref, out1_ref, out2_ref, out3_ref)):
+        out_ref[...] = total_ref[pl.ds(d * (n_class // NEAR), n_class // NEAR)].astype(out_ref.dtype)
+
+
+def insert_particles(place, offsets, row_kernel, col_kernel, pages, other_pages, n_class):
     n_pose, rows, _ = row_kernel.shape
     half = rows // 2
     out = (n_class, 3 * half, LCOLS)
     work = 2 * (pages.shape[0] - 1) * K_TOP * half * 2
     return pl.pallas_call(
-        functools.partial(particle_kernel, spread_over),
-        out_shape=jax.ShapeDtypeStruct(out, BF16),
+        particle_kernel,
+        out_shape=[jax.ShapeDtypeStruct((n_class // NEAR, *out[1:]), BF16)] * NEAR,
         in_specs=[pl.BlockSpec(memory_space=pltpu.SMEM)] + [pl.BlockSpec(memory_space=pl.ANY)] * 5,
-        out_specs=pl.BlockSpec(memory_space=pltpu.VMEM),
+        out_specs=[pl.BlockSpec(memory_space=pltpu.VMEM)] * NEAR,
         scratch_shapes=[
             pltpu.SMEM(offsets.shape, jnp.int32),
             pltpu.VMEM((n_pose, half, BAND), BF16),
             pltpu.VMEM(col_kernel.shape, BF16),
-            pltpu.VMEM((2, *pages.shape), BF16),
+            pltpu.VMEM((2, pages.shape[0] - 1, *pages.shape[1:]), BF16),
             pltpu.VMEM((n_pose, half, LANES), BF16),
             pltpu.VMEM(out, F32),
             pltpu.VMEM((IROWS, LANES), F32),
+            pltpu.VMEM((2, SMALL, LANES), BF16),
             pltpu.VMEM((2, SMALL, LANES), F32),
             pltpu.SMEM((2, SMALL, LANES), F32),
-            pltpu.SemaphoreType.DMA((6,)),
+            pltpu.SemaphoreType.DMA((8,)),
         ],
         cost_estimate=pl.CostEstimate(
             flops=work * (IROWS * 2 * LANES + 3 * LANES * LCOLS) * 8,
@@ -218,7 +225,7 @@
         ),
         compiler_params=pltpu.CompilerParams(vmem_limit_bytes=ALL_VMEM),
         name="insert_particles",
-    )(core, offsets, row_kernel, col_kernel, pages, other_pages)
+    )(place, offsets, row_kernel, col_kernel, pages, other_pages)
 
 
 def split_bf16(x):
@@ -291,14 +298,15 @@
     n = real.shape[0] // 2
     both = jnp.concatenate([real[:n] - imag[n:], real[n:] + imag[:n]], axis=1)
     out = dot3(split_bf16(both), (last_rows_ref[0], last_rows_ref[1]), NN)
-    out_ref[...] = out.astype(out_ref.dtype)
-
-
-def refine_class(planes, mix_rows, mix_cols, last_rows, last_cols):
+    for i in range(out_ref.shape[0]):
+        out_ref[i] = out.astype(out_ref.dtype)
+
+
+def refine_class(planes, mix_rows, mix_cols, last_rows, last_cols, n_copies):
     vmem = pl.BlockSpec(memory_space=pltpu.VMEM)
     return pl.pallas_call(
         refine_kernel,
-        out_shape=jax.ShapeDtypeStruct((last_cols.shape[1] // 2, BOX), BF16),
+        out_shape=jax.ShapeDtypeStruct((n_copies, last_cols.shape[1] // 2, BOX), BF16),
         in_specs=[vmem] * 5,
         out_specs=vmem,
         cost_estimate=pl.CostEstimate(flops=2 * 10**9, bytes_accessed=3 * 10**6, transcendentals=0),
@@ -322,25 +330,25 @@
 
 def added(parts):
     total = parts[0].astype(F32)
-    for i in range(1, parts.shape[0]):
+    for i in range(1, len(parts)):
         total = total + parts[i].astype(F32)
     return total
 
 
 def sum_at_owner(parts, axis):
     n = lax.axis_size(axis)
-    parts = parts.reshape(NEAR, n // NEAR, *parts.shape[1:])
-    parts = lax.all_to_all(parts, axis, 0, 0, axis_index_groups=neighbours(n, NEAR))
-    parts = added(parts).astype(BF16)
-    parts = lax.all_to_all(parts, axis, 0, 0, axis_index_groups=strided(n, NEAR))
-    return added(parts)
-
-
-def from_all(value, axis):
+    near = [parts[0], shift(parts[1], axis, 1), shift(parts[2], axis, 2), shift(parts[3], axis, -1)]
+    here = added(near).astype(BF16)
+    return added(lax.all_to_all(here, axis, 0, 0, axis_index_groups=strided(n, NEAR)))
+
+
+def from_all(copies, axis):
     n = lax.axis_size(axis)
-    far = lax.all_gather(value, axis, axis=0, axis_index_groups=strided(n, FAR))
-    every = lax.all_gather(far, axis, axis=0, axis_index_groups=neighbours(n, FAR))
-    return jnp.swapaxes(every, 0, 1).reshape(n, *value.shape)
+    far = lax.all_to_all(copies, axis, 0, 0, axis_index_groups=strided(n, NEAR))
+    every = lax.all_to_all(
+        jnp.broadcast_to(far, (NEAR, *far.shape)), axis, 0, 0, axis_index_groups=neighbours(n, NEAR)
+    )
+    return jnp.swapaxes(every, 0, 1).reshape(n, *copies.shape[1:])
 
 
 def per_device(spectra, defocus, classes, poses, probs, counts, offsets, row_kernel, col_kernel):
@@ -348,15 +356,17 @@
     group = lax.axis_size("sub") * lax.axis_size("pair")
     pages = prepare(counts, probs.T, defocus[None], classes.T, poses.T, spectra)
     other_pages = shift(pages, "pair", 1)
-    core = lax.axis_index("pair").reshape(1)
+    place = jnp.stack([lax.axis_index("pair"), lax.axis_index("parts") % NEAR])
     col_rows = jnp.swapaxes(col_kernel, 1, 2)
-    grids = insert_particles(core, offsets, row_kernel, col_rows, pages, other_pages, n_class, NEAR)
-    own = sum_at_owner(grids, "parts")
+    parts = insert_particles(place, offsets, row_kernel, col_rows, pages, other_pages, n_class)
+    own = sum_at_owner(parts, "parts")
     planes = lax.all_gather(own, ("sub", "pair"), axis=0, tiled=False)
     mix_rows, mix_cols, last_rows, last_cols = tables(group)
     mine = lax.dynamic_index_in_dim(jnp.asarray(last_cols), lax.axis_index(("sub", "pair")), 1, keepdims=False)
-    average = refine_class(planes, jnp.asarray(mix_rows), jnp.asarray(mix_cols), jnp.asarray(last_rows), mine)
-    return from_all(average, "parts").astype(F32)
+    copies = refine_class(
+        planes, jnp.asarray(mix_rows), jnp.asarray(mix_cols), jnp.asarray(last_rows), mine, n_class // NEAR
+    )
+    return from_all(copies, "parts").astype(F32)
 
 
 def solution(mesh):

time: 211 us -> 184 us (0.87)
  blocking collectives: 117 us -> 68.3 us
  starting transfers between devices: 42.5 us -> 55.5 us
  waiting for transfers between devices: 33.3 us -> 42.6 us
  other arithmetic: 0.92 us -> 3.48 us
  Pallas kernels: 13.4 us -> 11 us
    all_gather x2 -> x0, blocking collectives: 75 us -> none  [the longest x1 48.1 us: from_all(): lax.all_gather(far, axis, axis=0, axis_index_groups=neighbours(n, FAR))]
    ppermute x1 -> x4, starting transfers between devices: 1.95 us -> 51.2 us  [shift(): return lax.ppermute(value, axis, [(i, (i + by) % n) for i in range(n)])]
    all_to_all x1, starting transfers between devices: 40.5 us -> 4.32 us  [sum_at_owner(): lax.all_to_all(here, axis, 0, 0, axis_index_groups=strided(n, NEAR))]
    all_to_all x1 -> x2, blocking collectives: 28.4 us -> 54.6 us  [the longest x1 34.4 us: from_all(): far = lax.all_to_all(copies, axis, 0, 0, axis_index_groups=strided(n, NEAR))]
    ppermute x1 -> x4, waiting for transfers between devices: 2.26 us -> 12.4 us  [shift(): return lax.ppermute(value, axis, [(i, (i + by) % n) for i in range(n)])]
    convert_element_type x1 -> x2, other arithmetic: 0.11 us -> 2.83 us  [the longest x1 1.74 us: sum_at_owner(): here = added(near).astype(BF16)]
    pallas_call x2, Pallas kernels: 11.5 us -> 9.06 us  [the longest x1 5.69 us: insert_particles(): pl.pallas_call(particle_kernel, out_shape=[jax.ShapeDtypeStruct((n_class...]
  transfers between devices with their start and end apart: 2 -> 5, of which waited for: 2 -> 4; matrix products, arithmetic and copies ran while one was open for 0% -> 1% of each run, Pallas kernels for 0% -> 0%
where the time goes in v3:
time: 184 us; the launch traced here: 182 us
  blocking collectives  68.3 us (37%)
  starting transfers between devices  55.5 us (30%)
  waiting for transfers between devices  42.6 us (23%)
  Pallas kernels  11 us (6%)
  other arithmetic  3.48 us (2%)
    ppermute x4, starting transfers between devices, shift(): return lax.ppermute(value, axis, [(i, (i + by) % n) for i in range(n)])  51.2 us
    all_to_all x1, blocking collectives, from_all(): far = lax.all_to_all(copies, axis, 0, 0, axis_index_groups=strided(n, NEAR))  34.4 us
    all_to_all x1, waiting for transfers between devices, sum_at_owner(): lax.all_to_all(here, axis, 0, 0, axis_index_groups=strided(n, NEAR))  30.2 us
    all_to_all x1, blocking collectives, from_all(): lax.all_to_all(jnp.broadcast_to(far, (NEAR, *far.shape)), axis, 0, 0, axi...  20.2 us
    all_gather x1, blocking collectives, per_device(): planes = lax.all_gather(own, ('sub', 'pair'), axis=0, tiled=False)  13.7 us
    ppermute x4, waiting for transfers between devices, shift(): return lax.ppermute(value, axis, [(i, (i + by) % n) for i in range(n)])  12.4 us
    pallas_call x1, Pallas kernels, insert_particles(): pl.pallas_call(particle_kernel, out_shape=[jax.ShapeDtypeStruct((n_class...  5.69 us
    all_to_all x1, starting transfers between devices, sum_at_owner(): lax.all_to_all(here, axis, 0, 0, axis_index_groups=strided(n, NEAR))  4.32 us
  transfers between devices with their start and end apart: 5, of which 4 were waited for; matrix products, arithmetic and copies ran while one was open for 1% of the time, Pallas kernels for 0%

profile of v3, /device:TPU:40, one launch (start us, length us, event | category | flops | bytes accessed | tf_op | source)
XLA Modules:
  0.0 182.4 jit_solution(10576242233562390248)
XLA Ops:
  0.7 1.9 %prepare.1.own_in = bf16[17,128,128]{2,1,0:T(8,128)(2,1)} custom-call(s32[1]{0:T(128)S(6)} %copy.16.counts_in, bf16[4,16]{1,0:T(4,128)(2,1)} %bitcast.14, bf16[1,16]{1,0:T(2,128)(2,1)} %bitcast.15, s32[4,16]{1,0:T(4,128)} %bitcast.12, s32[4,16]{1,0:T(4,128)} %bitcast.13, bf16[16,128,128]{2,1,0:T(8,128)(2,1)} %spec_in.1), custom_call_target="tpu_custom_call" | custom-call | flops 1000000 | bytes 2000000 | tf_op jit(solution)/shard_map/prepare/pallas_call | solution.py:88
  2.6 2.0 %collective-permute-start = (bf16[17,128,128]{2,1,0:T(8,128)(2,1)}, bf16[17,128,128]{2,1,0:T(8,128)(2,1)}, u32[]{:S(2)}, u32[]{:S(2)}) collective-permute-start(bf16[17,128,128]{2,1,0:T(8,128)(2,1)} %prepare.1.own_in), channel_id=1, source_target_pairs={{0,1},{1,0},{2,3},{3,2},{4,5},{5,4},{6,7},{7,6},{8,9},{9,8},{10,11... | collective-permute-start | bytes 1671176 | tf_op jit(solution)/shard_map/ppermute | solution.py:320
  4.5 0.6 pad_add_fusion.place_ref
  5.1 1.6 collective-permute-done.other_in
  6.8 5.7 %insert_particles.1 = (bf16[8,96,128]{2,1,0:T(8,128)(2,1)}, bf16[8,96,128]{2,1,0:T(8,128)(2,1)}, bf16[8,96,128]{2,1,0:T(8,128)(2,1)}, bf16[8,96,128]{2,1,0:T(8,128)(2,1)}) custom-call(s32[2]{0:T(128)} %pad_add_fusion.place_ref, s32[32]{0:T(128)} %offsets_in.1, bf16[32,64,64]{2,1,0:T(8,128)(2,1)} %rk_in.1, bf16[32,64,128]{2,1,0:T(8,128)(2,1)} %bitcast.16, ...), custom_call_target="tpu_custom_call" | custom-call | flops 5368709120 | bytes 1572864 | tf_op jit(solution)/shard_map/insert_particles/pallas_call | solution.py:203
  12.5 8.1 %collective-permute-start.1 = (bf16[8,96,128]{2,1,0:T(8,128)(2,1)}, bf16[8,96,128]{2,1,0:T(8,128)(2,1)S(1)}, u32[]{:S(2)}, u32[]{:S(2)}) collective-permute-start(bf16[8,96,128]{2,1,0:T(8,128)(2,1)} %get-tuple-element.10), channel_id=1, source_target_pairs={{0,8},{8,16},{16,24},{24,32},{32,40},{40,48},{48,56},{56,64},{64,7... | collective-permute-start | bytes 589832 | tf_op jit(solution)/shard_map/ppermute | solution.py:320
  20.6 6.1 %collective-permute-start.2 = (bf16[8,96,128]{2,1,0:T(8,128)(2,1)}, bf16[8,96,128]{2,1,0:T(8,128)(2,1)S(1)}, u32[]{:S(2)}, u32[]{:S(2)}) collective-permute-start(bf16[8,96,128]{2,1,0:T(8,128)(2,1)} %get-tuple-element.11), channel_id=1, source_target_pairs={{0,16},{8,24},{16,32},{24,40},{32,48},{40,56},{48,64},{56,72},{64,... | collective-permute-start | bytes 589832 | tf_op jit(solution)/shard_map/ppermute | solution.py:320
  26.6 35.1 %collective-permute-start.3 = (bf16[8,96,128]{2,1,0:T(8,128)(2,1)}, bf16[8,96,128]{2,1,0:T(8,128)(2,1)S(1)}, u32[]{:S(2)}, u32[]{:S(2)}) collective-permute-start(bf16[8,96,128]{2,1,0:T(8,128)(2,1)} %get-tuple-element.12), channel_id=1, source_target_pairs={{0,248},{8,0},{16,8},{24,16},{32,24},{40,32},{48,40},{56,48},{64,5... | collective-permute-start | bytes 589832 | tf_op jit(solution)/shard_map/ppermute | solution.py:320
  61.7 2.2 %collective-permute-done.1 = bf16[8,96,128]{2,1,0:T(8,128)(2,1)S(1)} collective-permute-done((bf16[8,96,128]{2,1,0:T(8,128)(2,1)}, bf16[8,96,128]{2,1,0:T(8,128)(2,1)S(1)}, u32[]{:S(2)}, u32[]{:S(2)}) %collective-permute-start.1) | collective-permute-done | bytes 196640 | tf_op jit(solution)/shard_map/ppermute | solution.py:320
  64.0 8.6 %collective-permute-done.2 = bf16[8,96,128]{2,1,0:T(8,128)(2,1)S(1)} collective-permute-done((bf16[8,96,128]{2,1,0:T(8,128)(2,1)}, bf16[8,96,128]{2,1,0:T(8,128)(2,1)S(1)}, u32[]{:S(2)}, u32[]{:S(2)}) %collective-permute-start.2) | collective-permute-done | bytes 196640 | tf_op jit(solution)/shard_map/ppermute | solution.py:320
  72.6 0.0 collective-permute-done.3
  72.6 0.0 copy-start.2
  72.6 1.7 add_convert_fusion
  74.3 0.0 copy-start
  74.3 0.0 copy-start.1
  74.3 4.3 %all-to-all-start = ((bf16[8,96,128]{2,1,0:T(8,128)(2,1)}), bf16[8,96,128]{2,1,0:T(8,128)(2,1)S(1)}, u32[]{:S(2)}, u32[]{:S(2)}) async-start(bf16[8,96,128]{2,1,0:T(8,128)(2,1)} %add_convert_fusion), calls=%async_computation | async-start | bytes 393216 | tf_op jit(solution)/shard_map/all_to_all | solution.py:342
  78.6 0.8 dynamic-slice_bitcast_fusion.last_cols_ref
  79.4 30.2 %all-to-all-done = bf16[8,96,128]{2,1,0:T(8,128)(2,1)S(1)} async-done(((bf16[8,96,128]{2,1,0:T(8,128)(2,1)}), bf16[8,96,128]{2,1,0:T(8,128)(2,1)S(1)}, u32[]{:S(2)}, u32[]{:S(2)}) %all-to-all-start) | async-done | bytes 196640 | tf_op jit(solution)/shard_map/all_to_all | solution.py:342
  109.6 13.7 %all_gather.4.planes_ref = f32[8,96,128]{2,1,0:T(8,128)S(1)} all-gather(f32[1,96,128]{2,1,0:T(8,128)S(1)} %convert_add_fusion), channel_id=1, replica_groups=mesh['groups'=2,'parts'=32,'sub'=4,'pair'=2] {'sub','pair'}, dimensions={0}, use_global_device_ids=true | all-gather | bytes 442368 | tf_op jit(solution)/shard_map/all_gather | solution.py:363
  123.3 0.0 copy-done.2
  123.3 0.0 copy-done
  123.3 0.0 copy-done.1
  123.3 3.4 %refine_class.1 = bf16[8,32,256]{2,1,0:T(8,128)(2,1)S(1)} custom-call(f32[8,96,128]{2,1,0:T(8,128)S(1)} %all_gather.4.planes_ref, bf16[2,256,512]{2,1,0:T(8,128)(2,1)S(1)} %copy-done, bf16[2,128,256]{2,1,0:T(8,128)(2,1)S(1)} %copy-done.2, bf16[2,512,256]{2,1,0:T(8,128)(2,1)S(1)} %copy-done.1, bf16[2,64,128]{2,1,0:T(8,128)(2,1)S(1)} %dynamic-slice_bitcast_fusion.last_cols_ref), custom_call_target="tpu_custom_call" | custom-call | flops 2000000000 | bytes 3000000 | tf_op jit(solution)/shard_map/refine_class/pallas_call | solution.py:307
  126.7 34.4 %all_to_all.15 = bf16[8,32,256]{2,1,0:T(8,128)(2,1)S(1)} all-to-all(bf16[8,32,256]{2,1,0:T(8,128)(2,1)S(1)} %refine_class.1), channel_id=1, replica_groups={{0,32,64,96,128,160,192,224},{8,40,72,104,136,168,200,232},{16,48,80,11..., dimensions={0} | all-to-all | bytes 262144 | tf_op jit(solution)/shard_map/all_to_all | solution.py:347
  161.1 20.2 %all_to_all.16 = bf16[4,8,32,256]{3,2,1,0:T(8,128)(2,1)S(1)} all-to-all(bf16[4,8,32,256]{3,2,1,0:T(8,128)(2,1)S(1)} %broadcast_in_dim.7), channel_id=1, replica_groups={{0,8,16,24},{32,40,48,56},{64,72,80,88},{96,104,112,120},{128,136,144,1..., dimensions={0} | all-to-all | bytes 1048576 | tf_op jit(solution)/shard_map/all_to_all | solution.py:348
  181.3 1.1 copy_convert_fusion
  (2 shorter events, 0.1 us)
Async XLA Ops:
  2.6 4.2 %collective-permute-start = (bf16[17,128,128]{2,1,0:T(8,128)(2,1)}, bf16[17,128,128]{2,1,0:T(8,128)(2,1)}, u32[]{:S(2)}, u32[]{:S(2)}) collective-permute-start(bf16[17,128,128]{2,1,0:T(8,128)(2,1)} %prepare.1.own_in), channel_id=1, source_target_pairs={{0,1},{1,0},{2,3},{3,2},{4,5},{5,4},{6,7},{7,6},{8,9},{9,8},{10,11... | collective-permute-start | bytes 1671176 | tf_op jit(solution)/shard_map/ppermute | solution.py:320
  12.5 51.5 %collective-permute-start.1 = (bf16[8,96,128]{2,1,0:T(8,128)(2,1)}, bf16[8,96,128]{2,1,0:T(8,128)(2,1)S(1)}, u32[]{:S(2)}, u32[]{:S(2)}) collective-permute-start(bf16[8,96,128]{2,1,0:T(8,128)(2,1)} %get-tuple-element.10), channel_id=1, source_target_pairs={{0,8},{8,16},{16,24},{24,32},{32,40},{40,48},{48,56},{56,64},{64,7... | collective-permute-start | bytes 589832 | tf_op jit(solution)/shard_map/ppermute | solution.py:320
  20.6 52.0 %collective-permute-start.2 = (bf16[8,96,128]{2,1,0:T(8,128)(2,1)}, bf16[8,96,128]{2,1,0:T(8,128)(2,1)S(1)}, u32[]{:S(2)}, u32[]{:S(2)}) collective-permute-start(bf16[8,96,128]{2,1,0:T(8,128)(2,1)} %get-tuple-element.11), channel_id=1, source_target_pairs={{0,16},{8,24},{16,32},{24,40},{32,48},{40,56},{48,64},{56,72},{64,... | collective-permute-start | bytes 589832 | tf_op jit(solution)/shard_map/ppermute | solution.py:320
  26.6 45.9 %collective-permute-start.3 = (bf16[8,96,128]{2,1,0:T(8,128)(2,1)}, bf16[8,96,128]{2,1,0:T(8,128)(2,1)S(1)}, u32[]{:S(2)}, u32[]{:S(2)}) collective-permute-start(bf16[8,96,128]{2,1,0:T(8,128)(2,1)} %get-tuple-element.12), channel_id=1, source_target_pairs={{0,248},{8,0},{16,8},{24,16},{32,24},{40,32},{48,40},{56,48},{64,5... | collective-permute-start | bytes 589832 | tf_op jit(solution)/shard_map/ppermute | solution.py:320
  72.6 50.7 %copy-start.2 = (bf16[2,128,256]{2,1,0:T(8,128)(2,1)S(1)}, bf16[2,128,256]{2,1,0:T(8,128)(2,1)}, u32[]{:S(2)}) copy-start(bf16[2,128,256]{2,1,0:T(8,128)(2,1)} %constant.43.clone.mix_cols_ref) | copy-start | bytes 393220
  74.3 49.0 %copy-start = (bf16[2,256,512]{2,1,0:T(8,128)(2,1)S(1)}, bf16[2,256,512]{2,1,0:T(8,128)(2,1)}, u32[]{:S(2)}) copy-start(bf16[2,256,512]{2,1,0:T(8,128)(2,1)} %constant.42.clone.mix_rows_ref) | copy-start | bytes 1572868
  74.3 49.0 %copy-start.1 = (bf16[2,512,256]{2,1,0:T(8,128)(2,1)S(1)}, bf16[2,512,256]{2,1,0:T(8,128)(2,1)}, u32[]{:S(2)}) copy-start(bf16[2,512,256]{2,1,0:T(8,128)(2,1)} %constant.44.clone.last_rows_ref) | copy-start | bytes 1572868
  74.3 35.2 %all-to-all-start = ((bf16[8,96,128]{2,1,0:T(8,128)(2,1)}), bf16[8,96,128]{2,1,0:T(8,128)(2,1)S(1)}, u32[]{:S(2)}, u32[]{:S(2)}) async-start(bf16[8,96,128]{2,1,0:T(8,128)(2,1)} %add_convert_fusion), calls=%async_computation | async-start | bytes 393216 | tf_op jit(solution)/shard_map/all_to_all | solution.py:342

commit v4 on v3

--- a/solution.py
+++ b/solution.py
@@ -114,7 +114,7 @@
     n_class = total_ref.shape[0]
     n_pose, half = placed_ref.shape[0], placed_ref.shape[1]
     first_row = pl.multiple_of(place_ref[0] * half, half)
-    up = NEAR - place_ref[1]
+    here = place_ref[1]
     copies = start_all(
         [
             (own_in.at[n_slots, pl.ds(0, SMALL)], page_ref.at[0]),
@@ -129,8 +129,10 @@
     )
     lane = lax.broadcasted_iota(jnp.int32, (1, LANES), 1)
     low = lane < ICOLS
-    row_freq = (lax.broadcasted_iota(jnp.int32, (IROWS, LANES), 0) - IROWS // 2).astype(F32)
-    col_freq = (lax.broadcasted_iota(jnp.int32, (IROWS, LANES), 1) & (ICOLS - 1)).astype(F32)
+    packed = (IROWS // 2, LANES)
+    row_freq = lax.broadcasted_iota(jnp.int32, packed, 0) - jnp.where(low, IROWS // 2, 0)
+    row_freq = row_freq.astype(F32)
+    col_freq = (lax.broadcasted_iota(jnp.int32, packed, 1) & (ICOLS - 1)).astype(F32)
     radius_ref[...] = (row_freq * row_freq + col_freq * col_freq) * (10.0 / (ICOLS * ICOLS))
     total_ref[...] = jnp.zeros_like(total_ref)
     copies[0].wait()
@@ -169,6 +171,8 @@
             for term in SINE[-2::-1]:
                 s = s * z + term
             ctf = s * r * (1.0 - 2.0 * k * k)
+            turned = pltpu.roll(ctf, ICOLS, 1)
+            ctf = jnp.concatenate([jnp.where(low, ctf, turned), jnp.where(low, turned, ctf)], axis=0)
             data = (ctf * pages_ref[shard, n].astype(F32)).astype(BF16)
             power = jnp.where(low, ctf * ctf, 0.0).astype(BF16)
             planes = jnp.concatenate([data, power], axis=1)
@@ -185,7 +189,8 @@
                 cols = jnp.concatenate([cols, cols], axis=0)
                 spread = lax.dot_general(stacked, cols, NN, preferred_element_type=F32)
                 c = pick(shard, CLASSES + j, n)
-                sums.append((((c + up) % NEAR) * (n_class // NEAR) + c // NEAR, spread))
+                d = (c + n_class - here) % NEAR
+                sums.append((d * (n_class // NEAR) + c // NEAR, spread))
         for c, spread in sums:
             total_ref[c] += spread
         return carry
@@ -212,7 +217,7 @@
             pltpu.VMEM((2, pages.shape[0] - 1, *pages.shape[1:]), BF16),
             pltpu.VMEM((n_pose, half, LANES), BF16),
             pltpu.VMEM(out, F32),
-            pltpu.VMEM((IROWS, LANES), F32),
+            pltpu.VMEM((IROWS // 2, LANES), F32),
             pltpu.VMEM((2, SMALL, LANES), BF16),
             pltpu.VMEM((2, SMALL, LANES), F32),
             pltpu.SMEM((2, SMALL, LANES), F32),
@@ -320,10 +325,6 @@
     return lax.ppermute(value, axis, [(i, (i + by) % n) for i in range(n)])
 
 
-def neighbours(n, size):
-    return [[first + i for i in range(size)] for first in range(0, n, size)]
-
-
 def strided(n, stride):
     return [list(range(first, n, stride)) for first in range(stride)]
 
@@ -335,20 +336,51 @@
     return total
 
 
+def collect_kernel(a_ref, b_ref, c_ref, d_ref, out_ref):
+    out_ref[...] = added([a_ref[...], b_ref[...], c_ref[...], d_ref[...]]).astype(out_ref.dtype)
+
+
+def collect(parts):
+    vmem = pl.BlockSpec(memory_space=pltpu.VMEM)
+    return pl.pallas_call(
+        collect_kernel,
+        out_shape=jax.ShapeDtypeStruct(parts[0].shape, BF16),
+        in_specs=[vmem] * NEAR,
+        out_specs=vmem,
+        cost_estimate=pl.CostEstimate(flops=10**6, bytes_accessed=10**6, transcendentals=0),
+        compiler_params=pltpu.CompilerParams(vmem_limit_bytes=8 * 2**20),
+        name="collect",
+    )(*parts)
+
+
 def sum_at_owner(parts, axis):
+    here = collect([parts[0], shift(parts[1], axis, 1), shift(parts[2], axis, 2), shift(parts[3], axis, -1)])
+    return added(lax.all_to_all(here, axis, 0, 0, axis_index_groups=strided(lax.axis_size(axis), NEAR)))
+
+
+def place_kernel(place_ref, own_ref, *refs):
+    out_ref = refs[-1]
+    n_class = out_ref.shape[0]
+    for ref, d in zip((own_ref, *refs[:-1]), (0, 1, 2, -1)):
+        first = (place_ref[1] + d + n_class) % NEAR
+        for i in range(own_ref.shape[0]):
+            out_ref[NEAR * i + first] = ref[i].astype(F32)
+
+
+def from_all(copies, axis, place):
     n = lax.axis_size(axis)
-    near = [parts[0], shift(parts[1], axis, 1), shift(parts[2], axis, 2), shift(parts[3], axis, -1)]
-    here = added(near).astype(BF16)
-    return added(lax.all_to_all(here, axis, 0, 0, axis_index_groups=strided(n, NEAR)))
-
-
-def from_all(copies, axis):
-    n = lax.axis_size(axis)
-    far = lax.all_to_all(copies, axis, 0, 0, axis_index_groups=strided(n, NEAR))
-    every = lax.all_to_all(
-        jnp.broadcast_to(far, (NEAR, *far.shape)), axis, 0, 0, axis_index_groups=neighbours(n, NEAR)
-    )
-    return jnp.swapaxes(every, 0, 1).reshape(n, *copies.shape[1:])
+    own = lax.all_to_all(copies, axis, 0, 0, axis_index_groups=strided(n, NEAR))
+    near = [shift(own, axis, -1), shift(own, axis, -2), shift(own, axis, 1)]
+    vmem = pl.BlockSpec(memory_space=pltpu.VMEM)
+    return pl.pallas_call(
+        place_kernel,
+        out_shape=jax.ShapeDtypeStruct((n, *copies.shape[1:]), F32),
+        in_specs=[pl.BlockSpec(memory_space=pltpu.SMEM)] + [vmem] * NEAR,
+        out_specs=vmem,
+        cost_estimate=pl.CostEstimate(flops=10**6, bytes_accessed=2 * 10**6, transcendentals=0),
+        compiler_params=pltpu.CompilerParams(vmem_limit_bytes=16 * 2**20),
+        name="place_averages",
+    )(place, own, *near)
 
 
 def per_device(spectra, defocus, classes, poses, probs, counts, offsets, row_kernel, col_kernel):
@@ -356,17 +388,16 @@
     group = lax.axis_size("sub") * lax.axis_size("pair")
     pages = prepare(counts, probs.T, defocus[None], classes.T, poses.T, spectra)
     other_pages = shift(pages, "pair", 1)
-    place = jnp.stack([lax.axis_index("pair"), lax.axis_index("parts") % NEAR])
+    place = jnp.stack([lax.axis_index("pair"), lax.axis_index("parts")])
     col_rows = jnp.swapaxes(col_kernel, 1, 2)
     parts = insert_particles(place, offsets, row_kernel, col_rows, pages, other_pages, n_class)
-    own = sum_at_owner(parts, "parts")
-    planes = lax.all_gather(own, ("sub", "pair"), axis=0, tiled=False)
+    planes = lax.all_gather(sum_at_owner(parts, "parts"), ("sub", "pair"), axis=0, tiled=False)
     mix_rows, mix_cols, last_rows, last_cols = tables(group)
     mine = lax.dynamic_index_in_dim(jnp.asarray(last_cols), lax.axis_index(("sub", "pair")), 1, keepdims=False)
     copies = refine_class(
         planes, jnp.asarray(mix_rows), jnp.asarray(mix_cols), jnp.asarray(last_rows), mine, n_class // NEAR
     )
-    return from_all(copies, "parts").astype(F32)
+    return from_all(copies, "parts", place)
 
 
 def solution(mesh):

time: 184 us -> 182 us (0.989)
  blocking collectives: 68.3 us -> 45.2 us
  starting transfers between devices: 55.5 us -> 66.2 us
  waiting for transfers between devices: 42.6 us -> 50.1 us
  Pallas kernels: 11 us -> 16 us
  other arithmetic: 3.48 us -> 0.64 us
    all_to_all x2 -> x1, blocking collectives: 54.6 us -> 31.5 us  [from_all(): own = lax.all_to_all(copies, axis, 0, 0, axis_index_groups=strided(n, NEAR))]
    ppermute x4 -> x7, starting transfers between devices: 51.2 us -> 62.5 us  [shift(): return lax.ppermute(value, axis, [(i, (i + by) % n) for i in range(n)])]
    ppermute x4 -> x7, waiting for transfers between devices: 12.4 us -> 17.1 us  [shift(): return lax.ppermute(value, axis, [(i, (i + by) % n) for i in range(n)])]
    all_to_all x1, waiting for transfers between devices: 30.2 us -> 33 us  [sum_at_owner(): lax.all_to_all(here, axis, 0, 0, axis_index_groups=strided(lax.axis_size(...]
    convert_element_type x2 -> x0, other arithmetic: 2.83 us -> none  [the longest x1 1.74 us: sum_at_owner(): here = added(near).astype(BF16)]
    pallas_call x1, Pallas kernels: 5.69 us -> 8.42 us  [insert_particles(): pl.pallas_call(particle_kernel, out_shape=[jax.ShapeDtypeStruct((n_class...]
    pallas_call x0 -> x2, Pallas kernels: none -> 2.36 us  [the longest x1 1.59 us: from_all(): pl.pallas_call(place_kernel, out_shape=jax.ShapeDtypeStruct((n, *copies.s...]
  transfers between devices with their start and end apart: 5 -> 8, of which waited for: 4 -> 6; matrix products, arithmetic and copies ran while one was open for 1% -> 1% of each run, Pallas kernels for 0% -> 0%
where the time goes in v4:
time: 182 us; the launch traced here: 181 us
  starting transfers between devices  66.2 us (36%)
  waiting for transfers between devices  50.1 us (28%)
  blocking collectives  45.2 us (25%)
  Pallas kernels  16 us (9%)
    ppermute x7, starting transfers between devices, shift(): return lax.ppermute(value, axis, [(i, (i + by) % n) for i in range(n)])  62.5 us
    all_to_all x1, waiting for transfers between devices, sum_at_owner(): lax.all_to_all(here, axis, 0, 0, axis_index_groups=strided(lax.axis_size(...  33 us
    all_to_all x1, blocking collectives, from_all(): own = lax.all_to_all(copies, axis, 0, 0, axis_index_groups=strided(n, NEAR))  31.5 us
    ppermute x7, waiting for transfers between devices, shift(): return lax.ppermute(value, axis, [(i, (i + by) % n) for i in range(n)])  17.1 us
    all_gather x1, blocking collectives, per_device(): lax.all_gather(sum_at_owner(parts, 'parts'), ('sub', 'pair'), axis=0, til...  13.7 us
    pallas_call x1, Pallas kernels, insert_particles(): pl.pallas_call(particle_kernel, out_shape=[jax.ShapeDtypeStruct((n_class...  8.42 us
    all_to_all x1, starting transfers between devices, sum_at_owner(): lax.all_to_all(here, axis, 0, 0, axis_index_groups=strided(lax.axis_size(...  3.73 us
  transfers between devices with their start and end apart: 8, of which 6 were waited for; matrix products, arithmetic and copies ran while one was open for 1% of the time, Pallas kernels for 0%

profile of v4, /device:TPU:40, one launch (start us, length us, event | category | flops | bytes accessed | tf_op | source)
XLA Modules:
  0.0 180.8 jit_solution(13611287869491918537)
XLA Ops:
  0.7 1.9 %prepare.1.own_in = bf16[17,128,128]{2,1,0:T(8,128)(2,1)} custom-call(s32[1]{0:T(128)S(6)} %copy.14.counts_in, bf16[4,16]{1,0:T(4,128)(2,1)} %bitcast.11, bf16[1,16]{1,0:T(2,128)(2,1)} %bitcast.12, s32[4,16]{1,0:T(4,128)} %bitcast.9, s32[4,16]{1,0:T(4,128)} %bitcast.10, bf16[16,128,128]{2,1,0:T(8,128)(2,1)} %spec_in.1), custom_call_target="tpu_custom_call" | custom-call | flops 1000000 | bytes 2000000 | tf_op jit(solution)/shard_map/prepare/pallas_call | solution.py:88
  2.6 2.0 %collective-permute-start = (bf16[17,128,128]{2,1,0:T(8,128)(2,1)}, bf16[17,128,128]{2,1,0:T(8,128)(2,1)}, u32[]{:S(2)}, u32[]{:S(2)}) collective-permute-start(bf16[17,128,128]{2,1,0:T(8,128)(2,1)} %prepare.1.own_in), channel_id=1, source_target_pairs={{0,1},{1,0},{2,3},{3,2},{4,5},{5,4},{6,7},{7,6},{8,9},{9,8},{10,11... | collective-permute-start | bytes 1671176 | tf_op jit(solution)/shard_map/ppermute | solution.py:325
  4.5 0.6 pad_add_fusion.place_ref
  5.1 1.7 collective-permute-done.other_in
  6.8 8.4 %insert_particles.1 = (bf16[8,96,128]{2,1,0:T(8,128)(2,1)}, bf16[8,96,128]{2,1,0:T(8,128)(2,1)}, bf16[8,96,128]{2,1,0:T(8,128)(2,1)}, bf16[8,96,128]{2,1,0:T(8,128)(2,1)}) custom-call(s32[2]{0:T(128)} %pad_add_fusion.place_ref, s32[32]{0:T(128)} %offsets_in.1, bf16[32,64,64]{2,1,0:T(8,128)(2,1)} %rk_in.1, bf16[32,64,128]{2,1,0:T(8,128)(2,1)} %bitcast.13, ...), custom_call_target="tpu_custom_call" | custom-call | flops 5368709120 | bytes 1572864 | tf_op jit(solution)/shard_map/insert_particles/pallas_call | solution.py:208
  15.2 2.1 %collective-permute-start.1 = (bf16[8,96,128]{2,1,0:T(8,128)(2,1)}, bf16[8,96,128]{2,1,0:T(8,128)(2,1)S(1)}, u32[]{:S(2)}, u32[]{:S(2)}) collective-permute-start(bf16[8,96,128]{2,1,0:T(8,128)(2,1)} %get-tuple-element.10), channel_id=1, source_target_pairs={{0,8},{8,16},{16,24},{24,32},{32,40},{40,48},{48,56},{56,64},{64,7... | collective-permute-start | bytes 589832 | tf_op jit(solution)/shard_map/ppermute | solution.py:325
  17.3 11.3 %collective-permute-start.2 = (bf16[8,96,128]{2,1,0:T(8,128)(2,1)}, bf16[8,96,128]{2,1,0:T(8,128)(2,1)S(1)}, u32[]{:S(2)}, u32[]{:S(2)}) collective-permute-start(bf16[8,96,128]{2,1,0:T(8,128)(2,1)} %get-tuple-element.11), channel_id=1, source_target_pairs={{0,16},{8,24},{16,32},{24,40},{32,48},{40,56},{48,64},{56,72},{64,... | collective-permute-start | bytes 589832 | tf_op jit(solution)/shard_map/ppermute | solution.py:325
  28.6 35.8 %collective-permute-start.3 = (bf16[8,96,128]{2,1,0:T(8,128)(2,1)}, bf16[8,96,128]{2,1,0:T(8,128)(2,1)S(1)}, u32[]{:S(2)}, u32[]{:S(2)}) collective-permute-start(bf16[8,96,128]{2,1,0:T(8,128)(2,1)} %get-tuple-element.12), channel_id=1, source_target_pairs={{0,248},{8,0},{16,8},{24,16},{32,24},{40,32},{48,40},{56,48},{64,5... | collective-permute-start | bytes 589832 | tf_op jit(solution)/shard_map/ppermute | solution.py:325
  64.5 2.0 %collective-permute-done.1.b_ref = bf16[8,96,128]{2,1,0:T(8,128)(2,1)S(1)} collective-permute-done((bf16[8,96,128]{2,1,0:T(8,128)(2,1)}, bf16[8,96,128]{2,1,0:T(8,128)(2,1)S(1)}, u32[]{:S(2)}, u32[]{:S(2)}) %collective-permute-start.1) | collective-permute-done | bytes 196640 | tf_op jit(solution)/shard_map/ppermute | solution.py:325
  66.5 9.1 %collective-permute-done.2.c_ref = bf16[8,96,128]{2,1,0:T(8,128)(2,1)S(1)} collective-permute-done((bf16[8,96,128]{2,1,0:T(8,128)(2,1)}, bf16[8,96,128]{2,1,0:T(8,128)(2,1)S(1)}, u32[]{:S(2)}, u32[]{:S(2)}) %collective-permute-start.2) | collective-permute-done | bytes 196640 | tf_op jit(solution)/shard_map/ppermute | solution.py:325
  75.6 0.0 collective-permute-done.3.d_ref
  75.6 0.0 copy-start
  75.6 0.9 copy-done
  76.5 0.8 collect.1
  77.3 3.7 %all-to-all-start = ((bf16[8,96,128]{2,1,0:T(8,128)(2,1)}), bf16[8,96,128]{2,1,0:T(8,128)(2,1)S(1)}, u32[]{:S(2)}, u32[]{:S(2)}) async-start(bf16[8,96,128]{2,1,0:T(8,128)(2,1)} %collect.1), calls=%async_computation | async-start | bytes 393216 | tf_op jit(solution)/shard_map/all_to_all | solution.py:358
  81.1 0.8 dynamic-slice_bitcast_fusion.last_cols_ref
  81.8 33.0 %all-to-all-done = bf16[8,96,128]{2,1,0:T(8,128)(2,1)S(1)} async-done(((bf16[8,96,128]{2,1,0:T(8,128)(2,1)}), bf16[8,96,128]{2,1,0:T(8,128)(2,1)S(1)}, u32[]{:S(2)}, u32[]{:S(2)}) %all-to-all-start) | async-done | bytes 196640 | tf_op jit(solution)/shard_map/all_to_all | solution.py:358
  114.9 13.7 %all_gather.4.planes_ref = f32[8,96,128]{2,1,0:T(8,128)S(1)} all-gather(f32[1,96,128]{2,1,0:T(8,128)S(1)} %convert_add_fusion), channel_id=1, replica_groups=mesh['groups'=2,'parts'=32,'sub'=4,'pair'=2] {'sub','pair'}, dimensions={0}, use_global_device_ids=true | all-gather | bytes 442368 | tf_op jit(solution)/shard_map/all_gather | solution.py:394
  128.6 0.0 copy-done.4
  128.6 0.0 copy-done.2
  128.6 0.0 copy-done.3
  128.6 3.4 %refine_class.1 = bf16[8,32,256]{2,1,0:T(8,128)(2,1)S(1)} custom-call(f32[8,96,128]{2,1,0:T(8,128)S(1)} %all_gather.4.planes_ref, bf16[2,256,512]{2,1,0:T(8,128)(2,1)S(1)} %copy-done.2, bf16[2,128,256]{2,1,0:T(8,128)(2,1)S(1)} %copy-done.4, bf16[2,512,256]{2,1,0:T(8,128)(2,1)S(1)} %copy-done.3, bf16[2,64,128]{2,1,0:T(8,128)(2,1)S(1)} %dynamic-slice_bitcast_fusion.last_cols_ref), custom_call_target="tpu_custom_call" | custom-call | flops 2000000000 | bytes 3000000 | tf_op jit(solution)/shard_map/refine_class/pallas_call | solution.py:312
  132.0 0.0 copy-start.1
  132.0 31.5 %all_to_all.10.own_ref = bf16[8,32,256]{2,1,0:T(8,128)(2,1)S(1)} all-to-all(bf16[8,32,256]{2,1,0:T(8,128)(2,1)S(1)} %refine_class.1), channel_id=1, replica_groups={{0,32,64,96,128,160,192,224},{8,40,72,104,136,168,200,232},{16,48,80,11..., dimensions={0} | all-to-all | bytes 262144 | tf_op jit(solution)/shard_map/all_to_all | solution.py:372
  163.5 1.9 %collective-permute-start.4 = (bf16[8,32,256]{2,1,0:T(8,128)(2,1)S(1)}, bf16[8,32,256]{2,1,0:T(8,128)(2,1)S(1)}, u32[]{:S(2)}, u32[]{:S(2)}) collective-permute-start(bf16[8,32,256]{2,1,0:T(8,128)(2,1)S(1)} %all_to_all.10.own_ref), channel_id=1, source_target_pairs={{0,248},{8,0},{16,8},{24,16},{32,24},{40,32},{48,40},{56,48},{64,5... | collective-permute-start | bytes 393224 | tf_op jit(solution)/shard_map/ppermute | solution.py:325
  165.4 5.4 %collective-permute-start.5 = (bf16[8,32,256]{2,1,0:T(8,128)(2,1)S(1)}, bf16[8,32,256]{2,1,0:T(8,128)(2,1)S(1)}, u32[]{:S(2)}, u32[]{:S(2)}) collective-permute-start(bf16[8,32,256]{2,1,0:T(8,128)(2,1)S(1)} %all_to_all.10.own_ref), channel_id=1, source_target_pairs={{0,240},{8,248},{16,0},{24,8},{32,16},{40,24},{48,32},{56,40},{64,... | collective-permute-start | bytes 393224 | tf_op jit(solution)/shard_map/ppermute | solution.py:325
  170.9 4.0 %collective-permute-start.6 = (bf16[8,32,256]{2,1,0:T(8,128)(2,1)S(1)}, bf16[8,32,256]{2,1,0:T(8,128)(2,1)S(1)}, u32[]{:S(2)}, u32[]{:S(2)}) collective-permute-start(bf16[8,32,256]{2,1,0:T(8,128)(2,1)S(1)} %all_to_all.10.own_ref), channel_id=1, source_target_pairs={{0,8},{8,16},{16,24},{24,32},{32,40},{40,48},{48,56},{56,64},{64,7... | collective-permute-start | bytes 393224 | tf_op jit(solution)/shard_map/ppermute | solution.py:325
  174.8 0.0 collective-permute-done.4.refs_0_
  174.8 2.9 %collective-permute-done.5.refs_1_ = bf16[8,32,256]{2,1,0:T(8,128)(2,1)S(1)} collective-permute-done((bf16[8,32,256]{2,1,0:T(8,128)(2,1)S(1)}, bf16[8,32,256]{2,1,0:T(8,128)(2,1)S(1)}, u32[]{:S(2)}, u32[]{:S(2)}) %collective-permute-start.5) | collective-permute-done | bytes 131104 | tf_op jit(solution)/shard_map/ppermute | solution.py:325
  177.7 1.4 collective-permute-done.6.refs_2_
  179.2 0.0 copy-done.1
  179.2 1.6 place_averages.1
  (4 shorter events, 0.0 us)
Async XLA Ops:
  2.6 4.2 %collective-permute-start = (bf16[17,128,128]{2,1,0:T(8,128)(2,1)}, bf16[17,128,128]{2,1,0:T(8,128)(2,1)}, u32[]{:S(2)}, u32[]{:S(2)}) collective-permute-start(bf16[17,128,128]{2,1,0:T(8,128)(2,1)} %prepare.1.own_in), channel_id=1, source_target_pairs={{0,1},{1,0},{2,3},{3,2},{4,5},{5,4},{6,7},{7,6},{8,9},{9,8},{10,11... | collective-permute-start | bytes 1671176 | tf_op jit(solution)/shard_map/ppermute | solution.py:325
  15.2 51.3 %collective-permute-start.1 = (bf16[8,96,128]{2,1,0:T(8,128)(2,1)}, bf16[8,96,128]{2,1,0:T(8,128)(2,1)S(1)}, u32[]{:S(2)}, u32[]{:S(2)}) collective-permute-start(bf16[8,96,128]{2,1,0:T(8,128)(2,1)} %get-tuple-element.10), channel_id=1, source_target_pairs={{0,8},{8,16},{16,24},{24,32},{32,40},{40,48},{48,56},{56,64},{64,7... | collective-permute-start | bytes 589832 | tf_op jit(solution)/shard_map/ppermute | solution.py:325
  17.3 58.3 %collective-permute-start.2 = (bf16[8,96,128]{2,1,0:T(8,128)(2,1)}, bf16[8,96,128]{2,1,0:T(8,128)(2,1)S(1)}, u32[]{:S(2)}, u32[]{:S(2)}) collective-permute-start(bf16[8,96,128]{2,1,0:T(8,128)(2,1)} %get-tuple-element.11), channel_id=1, source_target_pairs={{0,16},{8,24},{16,32},{24,40},{32,48},{40,56},{48,64},{56,72},{64,... | collective-permute-start | bytes 589832 | tf_op jit(solution)/shard_map/ppermute | solution.py:325
  28.6 47.0 %collective-permute-start.3 = (bf16[8,96,128]{2,1,0:T(8,128)(2,1)}, bf16[8,96,128]{2,1,0:T(8,128)(2,1)S(1)}, u32[]{:S(2)}, u32[]{:S(2)}) collective-permute-start(bf16[8,96,128]{2,1,0:T(8,128)(2,1)} %get-tuple-element.12), channel_id=1, source_target_pairs={{0,248},{8,0},{16,8},{24,16},{32,24},{40,32},{48,40},{56,48},{64,5... | collective-permute-start | bytes 589832 | tf_op jit(solution)/shard_map/ppermute | solution.py:325
  75.6 0.9 copy-start
  76.5 52.1 %copy-start.4 = (bf16[2,128,256]{2,1,0:T(8,128)(2,1)S(1)}, bf16[2,128,256]{2,1,0:T(8,128)(2,1)}, u32[]{:S(2)}) copy-start(bf16[2,128,256]{2,1,0:T(8,128)(2,1)} %constant.31.clone.mix_cols_ref) | copy-start | bytes 393220
  77.3 51.3 %copy-start.2 = (bf16[2,256,512]{2,1,0:T(8,128)(2,1)S(1)}, bf16[2,256,512]{2,1,0:T(8,128)(2,1)}, u32[]{:S(2)}) copy-start(bf16[2,256,512]{2,1,0:T(8,128)(2,1)} %constant.30.clone.mix_rows_ref) | copy-start | bytes 1572868
  77.3 51.3 %copy-start.3 = (bf16[2,512,256]{2,1,0:T(8,128)(2,1)S(1)}, bf16[2,512,256]{2,1,0:T(8,128)(2,1)}, u32[]{:S(2)}) copy-start(bf16[2,512,256]{2,1,0:T(8,128)(2,1)} %constant.32.clone.last_rows_ref) | copy-start | bytes 1572868
  77.3 37.5 %all-to-all-start = ((bf16[8,96,128]{2,1,0:T(8,128)(2,1)}), bf16[8,96,128]{2,1,0:T(8,128)(2,1)S(1)}, u32[]{:S(2)}, u32[]{:S(2)}) async-start(bf16[8,96,128]{2,1,0:T(8,128)(2,1)} %collect.1), calls=%async_computation | async-start | bytes 393216 | tf_op jit(solution)/shard_map/all_to_all | solution.py:358
  132.0 47.2 %copy-start.1 = (s32[2]{0:T(128)S(1)}, s32[2]{0:T(128)}, u32[]{:S(2)}) copy-start(s32[2]{0:T(128)} %pad_add_fusion.place_ref) | copy-start | bytes 28
  163.5 11.4 %collective-permute-start.4 = (bf16[8,32,256]{2,1,0:T(8,128)(2,1)S(1)}, bf16[8,32,256]{2,1,0:T(8,128)(2,1)S(1)}, u32[]{:S(2)}, u32[]{:S(2)}) collective-permute-start(bf16[8,32,256]{2,1,0:T(8,128)(2,1)S(1)} %all_to_all.10.own_ref), channel_id=1, source_target_pairs={{0,248},{8,0},{16,8},{24,16},{32,24},{40,32},{48,40},{56,48},{64,5... | collective-permute-start | bytes 393224 | tf_op jit(solution)/shard_map/ppermute | solution.py:325
  165.4 12.3 %collective-permute-start.5 = (bf16[8,32,256]{2,1,0:T(8,128)(2,1)S(1)}, bf16[8,32,256]{2,1,0:T(8,128)(2,1)S(1)}, u32[]{:S(2)}, u32[]{:S(2)}) collective-permute-start(bf16[8,32,256]{2,1,0:T(8,128)(2,1)S(1)} %all_to_all.10.own_ref), channel_id=1, source_target_pairs={{0,240},{8,248},{16,0},{24,8},{32,16},{40,24},{48,32},{56,40},{64,... | collective-permute-start | bytes 393224 | tf_op jit(solution)/shard_map/ppermute | solution.py:325
  170.9 8.3 %collective-permute-start.6 = (bf16[8,32,256]{2,1,0:T(8,128)(2,1)S(1)}, bf16[8,32,256]{2,1,0:T(8,128)(2,1)S(1)}, u32[]{:S(2)}, u32[]{:S(2)}) collective-permute-start(bf16[8,32,256]{2,1,0:T(8,128)(2,1)S(1)} %all_to_all.10.own_ref), channel_id=1, source_target_pairs={{0,8},{8,16},{16,24},{24,32},{32,40},{40,48},{48,56},{56,64},{64,7... | collective-permute-start | bytes 393224 | tf_op jit(solution)/shard_map/ppermute | solution.py:325

commit v5 on v4

--- a/solution.py
+++ b/solution.py
@@ -107,7 +107,7 @@
 
 def particle_kernel(
     place_ref, offsets_in, rk_in, ck_in, own_in, other_in,
-    out0_ref, out1_ref, out2_ref, out3_ref,
+    out0_ref, out1_ref, out2_ref, out2b_ref, out3_ref,
     offsets_ref, rows_ref, cols_ref, pages_ref, placed_ref, total_ref, radius_ref, page_ref, small_ref, scalars_ref, sems,
 ):
     n_slots = pages_ref.shape[1]
@@ -196,20 +196,24 @@
         return carry
 
     lax.fori_loop(0, blocks[0] + blocks[1], step, 0)
-    for d, out_ref in enumerate((out0_ref, out1_ref, out2_ref, out3_ref)):
-        out_ref[...] = total_ref[pl.ds(d * (n_class // NEAR), n_class // NEAR)].astype(out_ref.dtype)
+    first = 0
+    for out_ref in (out0_ref, out1_ref, out2_ref, out2b_ref, out3_ref):
+        out_ref[...] = total_ref[first : first + out_ref.shape[0]].astype(out_ref.dtype)
+        first += out_ref.shape[0]
 
 
 def insert_particles(place, offsets, row_kernel, col_kernel, pages, other_pages, n_class):
     n_pose, rows, _ = row_kernel.shape
     half = rows // 2
     out = (n_class, 3 * half, LCOLS)
+    each = n_class // NEAR
+    sizes = (each, each, each // 2, each - each // 2, each)
     work = 2 * (pages.shape[0] - 1) * K_TOP * half * 2
     return pl.pallas_call(
         particle_kernel,
-        out_shape=[jax.ShapeDtypeStruct((n_class // NEAR, *out[1:]), BF16)] * NEAR,
+        out_shape=[jax.ShapeDtypeStruct((size, *out[1:]), BF16) for size in sizes],
         in_specs=[pl.BlockSpec(memory_space=pltpu.SMEM)] + [pl.BlockSpec(memory_space=pl.ANY)] * 5,
-        out_specs=[pl.BlockSpec(memory_space=pltpu.VMEM)] * NEAR,
+        out_specs=[pl.BlockSpec(memory_space=pltpu.VMEM)] * len(sizes),
         scratch_shapes=[
             pltpu.SMEM(offsets.shape, jnp.int32),
             pltpu.VMEM((n_pose, half, BAND), BF16),
@@ -336,16 +340,18 @@
     return total
 
 
-def collect_kernel(a_ref, b_ref, c_ref, d_ref, out_ref):
-    out_ref[...] = added([a_ref[...], b_ref[...], c_ref[...], d_ref[...]]).astype(out_ref.dtype)
-
-
-def collect(parts):
+def collect_kernel(a_ref, b_ref, low_ref, high_ref, d_ref, out_ref):
+    n_low = low_ref.shape[0]
+    out_ref[:n_low] = added([a_ref[:n_low], b_ref[:n_low], low_ref[...], d_ref[:n_low]]).astype(out_ref.dtype)
+    out_ref[n_low:] = added([a_ref[n_low:], b_ref[n_low:], high_ref[...], d_ref[n_low:]]).astype(out_ref.dtype)
+
+
+def collect(*parts):
     vmem = pl.BlockSpec(memory_space=pltpu.VMEM)
     return pl.pallas_call(
         collect_kernel,
         out_shape=jax.ShapeDtypeStruct(parts[0].shape, BF16),
-        in_specs=[vmem] * NEAR,
+        in_specs=[vmem] * len(parts),
         out_specs=vmem,
         cost_estimate=pl.CostEstimate(flops=10**6, bytes_accessed=10**6, transcendentals=0),
         compiler_params=pltpu.CompilerParams(vmem_limit_bytes=8 * 2**20),
@@ -354,7 +360,13 @@
 
 
 def sum_at_owner(parts, axis):
-    here = collect([parts[0], shift(parts[1], axis, 1), shift(parts[2], axis, 2), shift(parts[3], axis, -1)])
+    here = collect(
+        parts[0],
+        shift(parts[1], axis, 1),
+        shift(parts[2], axis, 2),
+        shift(parts[3], axis, -2),
+        shift(parts[4], axis, -1),
+    )
     return added(lax.all_to_all(here, axis, 0, 0, axis_index_groups=strided(lax.axis_size(axis), NEAR)))
 
 

time: 182 us -> 183 us (level)
  waiting for transfers between devices: 50.1 us -> 37.5 us
  blocking collectives: 45.2 us -> 53.7 us
  starting transfers between devices: 66.2 us -> 71.9 us
    all_to_all x1, blocking collectives: 31.5 us -> 40 us  [from_all(): own = lax.all_to_all(copies, axis, 0, 0, axis_index_groups=strided(n, NEAR))]
    ppermute x7 -> x8, waiting for transfers between devices: 17.1 us -> 10.4 us  [shift(): return lax.ppermute(value, axis, [(i, (i + by) % n) for i in range(n)])]
    all_to_all x1, waiting for transfers between devices: 33 us -> 27.1 us  [sum_at_owner(): lax.all_to_all(here, axis, 0, 0, axis_index_groups=strided(lax.axis_size(...]
    ppermute x7 -> x8, starting transfers between devices: 62.5 us -> 67 us  [shift(): return lax.ppermute(value, axis, [(i, (i + by) % n) for i in range(n)])]
  transfers between devices with their start and end apart: 8 -> 9, of which waited for: 6 -> 6; matrix products, arithmetic and copies ran while one was open for 1% -> 1% of each run, Pallas kernels for 0% -> 0%
where the time goes in v5:
time: 183 us
  starting transfers between devices  71.9 us (39%)
  blocking collectives  53.7 us (29%)
  waiting for transfers between devices  37.5 us (20%)
  Pallas kernels  17 us (9%)
    ppermute x8, starting transfers between devices, shift(): return lax.ppermute(value, axis, [(i, (i + by) % n) for i in range(n)])  67 us
    all_to_all x1, blocking collectives, from_all(): own = lax.all_to_all(copies, axis, 0, 0, axis_index_groups=strided(n, NEAR))  40 us
    all_to_all x1, waiting for transfers between devices, sum_at_owner(): lax.all_to_all(here, axis, 0, 0, axis_index_groups=strided(lax.axis_size(...  27.1 us
    all_gather x1, blocking collectives, per_device(): lax.all_gather(sum_at_owner(parts, 'parts'), ('sub', 'pair'), axis=0, til...  13.7 us
    ppermute x8, waiting for transfers between devices, shift(): return lax.ppermute(value, axis, [(i, (i + by) % n) for i in range(n)])  10.4 us
    pallas_call x1, Pallas kernels, insert_particles(): pl.pallas_call(particle_kernel, out_shape=[jax.ShapeDtypeStruct((size, *o...  9.33 us
    all_to_all x1, starting transfers between devices, sum_at_owner(): lax.all_to_all(here, axis, 0, 0, axis_index_groups=strided(lax.axis_size(...  4.84 us
  transfers between devices with their start and end apart: 9, of which 6 were waited for; matrix products, arithmetic and copies ran while one was open for 1% of the time, Pallas kernels for 0%

profile of v5, /device:TPU:40, one launch (start us, length us, event | category | flops | bytes accessed | tf_op | source)
XLA Modules:
  0.0 183.2 jit_solution(7256254017880296907)
XLA Ops:
  0.7 1.9 %prepare.1.own_in = bf16[17,128,128]{2,1,0:T(8,128)(2,1)} custom-call(s32[1]{0:T(128)S(6)} %copy.14.counts_in, bf16[4,16]{1,0:T(4,128)(2,1)} %bitcast.11, bf16[1,16]{1,0:T(2,128)(2,1)} %bitcast.12, s32[4,16]{1,0:T(4,128)} %bitcast.9, s32[4,16]{1,0:T(4,128)} %bitcast.10, bf16[16,128,128]{2,1,0:T(8,128)(2,1)} %spec_in.1), custom_call_target="tpu_custom_call" | custom-call | flops 1000000 | bytes 2000000 | tf_op jit(solution)/shard_map/prepare/pallas_call | solution.py:88
  2.6 2.0 %collective-permute-start = (bf16[17,128,128]{2,1,0:T(8,128)(2,1)}, bf16[17,128,128]{2,1,0:T(8,128)(2,1)}, u32[]{:S(2)}, u32[]{:S(2)}) collective-permute-start(bf16[17,128,128]{2,1,0:T(8,128)(2,1)} %prepare.1.own_in), channel_id=1, source_target_pairs={{0,1},{1,0},{2,3},{3,2},{4,5},{5,4},{6,7},{7,6},{8,9},{9,8},{10,11... | collective-permute-start | bytes 1671176 | tf_op jit(solution)/shard_map/ppermute | solution.py:329
  4.5 0.6 pad_add_fusion.place_ref
  5.2 1.6 collective-permute-done.other_in
  6.8 9.3 %insert_particles.1 = (bf16[8,96,128]{2,1,0:T(8,128)(2,1)}, bf16[8,96,128]{2,1,0:T(8,128)(2,1)}, bf16[4,96,128]{2,1,0:T(8,128)(2,1)}, bf16[4,96,128]{2,1,0:T(8,128)(2,1)}, bf16[8,96,128]{2,1,0:T(8,128)(2,1)}) custom-call(s32[2]{0:T(128)} %pad_add_fusion.place_ref, s32[32]{0:T(128)} %offsets_in.1, bf16[32,64,64]{2,1,0:T(8,128)(2,1)} %rk_in.1, ...), custom_call_target="tpu_custom_call" | custom-call | flops 5368709120 | bytes 1572864 | tf_op jit(solution)/shard_map/insert_particles/pallas_call | solution.py:212
  16.1 3.8 %collective-permute-start.1 = (bf16[8,96,128]{2,1,0:T(8,128)(2,1)}, bf16[8,96,128]{2,1,0:T(8,128)(2,1)S(1)}, u32[]{:S(2)}, u32[]{:S(2)}) collective-permute-start(bf16[8,96,128]{2,1,0:T(8,128)(2,1)} %get-tuple-element.11), channel_id=1, source_target_pairs={{0,8},{8,16},{16,24},{24,32},{32,40},{40,48},{48,56},{56,64},{64,7... | collective-permute-start | bytes 589832 | tf_op jit(solution)/shard_map/ppermute | solution.py:329
  20.0 43.4 %collective-permute-start.4 = (bf16[8,96,128]{2,1,0:T(8,128)(2,1)}, bf16[8,96,128]{2,1,0:T(8,128)(2,1)S(1)}, u32[]{:S(2)}, u32[]{:S(2)}) collective-permute-start(bf16[8,96,128]{2,1,0:T(8,128)(2,1)} %get-tuple-element.14), channel_id=1, source_target_pairs={{0,248},{8,0},{16,8},{24,16},{32,24},{40,32},{48,40},{56,48},{64,5... | collective-permute-start | bytes 589832 | tf_op jit(solution)/shard_map/ppermute | solution.py:329
  63.4 2.0 %collective-permute-start.2 = (bf16[4,96,128]{2,1,0:T(8,128)(2,1)}, bf16[4,96,128]{2,1,0:T(8,128)(2,1)S(1)}, u32[]{:S(2)}, u32[]{:S(2)}) collective-permute-start(bf16[4,96,128]{2,1,0:T(8,128)(2,1)} %get-tuple-element.12), channel_id=1, source_target_pairs={{0,16},{8,24},{16,32},{24,40},{32,48},{40,56},{48,64},{56,72},{64,... | collective-permute-start | bytes 294920 | tf_op jit(solution)/shard_map/ppermute | solution.py:329
  65.4 6.1 %collective-permute-start.3 = (bf16[4,96,128]{2,1,0:T(8,128)(2,1)}, bf16[4,96,128]{2,1,0:T(8,128)(2,1)S(1)}, u32[]{:S(2)}, u32[]{:S(2)}) collective-permute-start(bf16[4,96,128]{2,1,0:T(8,128)(2,1)} %get-tuple-element.13), channel_id=1, source_target_pairs={{0,240},{8,248},{16,0},{24,8},{32,16},{40,24},{48,32},{56,40},{64,... | collective-permute-start | bytes 294920 | tf_op jit(solution)/shard_map/ppermute | solution.py:329
  71.5 2.9 %collective-permute-done.2.low_ref = bf16[4,96,128]{2,1,0:T(8,128)(2,1)S(1)} collective-permute-done((bf16[4,96,128]{2,1,0:T(8,128)(2,1)}, bf16[4,96,128]{2,1,0:T(8,128)(2,1)S(1)}, u32[]{:S(2)}, u32[]{:S(2)}) %collective-permute-start.2) | collective-permute-done | bytes 98336 | tf_op jit(solution)/shard_map/ppermute | solution.py:329
  74.3 1.2 collective-permute-done.3.high_ref
  75.6 0.0 collective-permute-done.1.b_ref
  75.6 0.0 collective-permute-done.4.d_ref
  75.6 0.9 copy-done
  76.5 0.8 collect.1
  77.3 4.8 %all-to-all-start = ((bf16[8,96,128]{2,1,0:T(8,128)(2,1)}), bf16[8,96,128]{2,1,0:T(8,128)(2,1)S(1)}, u32[]{:S(2)}, u32[]{:S(2)}) async-start(bf16[8,96,128]{2,1,0:T(8,128)(2,1)} %collect.1), calls=%async_computation | async-start | bytes 393216 | tf_op jit(solution)/shard_map/all_to_all | solution.py:370
  82.1 0.8 dynamic-slice_bitcast_fusion.last_cols_ref
  82.9 27.1 %all-to-all-done = bf16[8,96,128]{2,1,0:T(8,128)(2,1)S(1)} async-done(((bf16[8,96,128]{2,1,0:T(8,128)(2,1)}), bf16[8,96,128]{2,1,0:T(8,128)(2,1)S(1)}, u32[]{:S(2)}, u32[]{:S(2)}) %all-to-all-start) | async-done | bytes 196640 | tf_op jit(solution)/shard_map/all_to_all | solution.py:370
  110.0 13.7 %all_gather.4.planes_ref = f32[8,96,128]{2,1,0:T(8,128)S(1)} all-gather(f32[1,96,128]{2,1,0:T(8,128)S(1)} %convert_add_fusion), channel_id=1, replica_groups=mesh['groups'=2,'parts'=32,'sub'=4,'pair'=2] {'sub','pair'}, dimensions={0}, use_global_device_ids=true | all-gather | bytes 442368 | tf_op jit(solution)/shard_map/all_gather | solution.py:406
  123.7 0.0 copy-done.4
  123.7 0.0 copy-done.2
  123.7 0.0 copy-done.3
  123.7 3.4 %refine_class.1 = bf16[8,32,256]{2,1,0:T(8,128)(2,1)S(1)} custom-call(f32[8,96,128]{2,1,0:T(8,128)S(1)} %all_gather.4.planes_ref, bf16[2,256,512]{2,1,0:T(8,128)(2,1)S(1)} %copy-done.2, bf16[2,128,256]{2,1,0:T(8,128)(2,1)S(1)} %copy-done.4, bf16[2,512,256]{2,1,0:T(8,128)(2,1)S(1)} %copy-done.3, bf16[2,64,128]{2,1,0:T(8,128)(2,1)S(1)} %dynamic-slice_bitcast_fusion.last_cols_ref), custom_call_target="tpu_custom_call" | custom-call | flops 2000000000 | bytes 3000000 | tf_op jit(solution)/shard_map/refine_class/pallas_call | solution.py:316
  127.1 40.0 %all_to_all.10.own_ref = bf16[8,32,256]{2,1,0:T(8,128)(2,1)S(1)} all-to-all(bf16[8,32,256]{2,1,0:T(8,128)(2,1)S(1)} %refine_class.1), channel_id=1, replica_groups={{0,32,64,96,128,160,192,224},{8,40,72,104,136,168,200,232},{16,48,80,11..., dimensions={0} | all-to-all | bytes 262144 | tf_op jit(solution)/shard_map/all_to_all | solution.py:384
  167.1 4.4 %collective-permute-start.5 = (bf16[8,32,256]{2,1,0:T(8,128)(2,1)S(1)}, bf16[8,32,256]{2,1,0:T(8,128)(2,1)S(1)}, u32[]{:S(2)}, u32[]{:S(2)}) collective-permute-start(bf16[8,32,256]{2,1,0:T(8,128)(2,1)S(1)} %all_to_all.10.own_ref), channel_id=1, source_target_pairs={{0,248},{8,0},{16,8},{24,16},{32,24},{40,32},{48,40},{56,48},{64,5... | collective-permute-start | bytes 393224 | tf_op jit(solution)/shard_map/ppermute | solution.py:329
  171.5 2.0 %collective-permute-start.6 = (bf16[8,32,256]{2,1,0:T(8,128)(2,1)S(1)}, bf16[8,32,256]{2,1,0:T(8,128)(2,1)S(1)}, u32[]{:S(2)}, u32[]{:S(2)}) collective-permute-start(bf16[8,32,256]{2,1,0:T(8,128)(2,1)S(1)} %all_to_all.10.own_ref), channel_id=1, source_target_pairs={{0,240},{8,248},{16,0},{24,8},{32,16},{40,24},{48,32},{56,40},{64,... | collective-permute-start | bytes 393224 | tf_op jit(solution)/shard_map/ppermute | solution.py:329
  173.5 3.4 %collective-permute-start.7 = (bf16[8,32,256]{2,1,0:T(8,128)(2,1)S(1)}, bf16[8,32,256]{2,1,0:T(8,128)(2,1)S(1)}, u32[]{:S(2)}, u32[]{:S(2)}) collective-permute-start(bf16[8,32,256]{2,1,0:T(8,128)(2,1)S(1)} %all_to_all.10.own_ref), channel_id=1, source_target_pairs={{0,8},{8,16},{16,24},{24,32},{32,40},{40,48},{48,56},{56,64},{64,7... | collective-permute-start | bytes 393224 | tf_op jit(solution)/shard_map/ppermute | solution.py:329
  176.9 0.0 collective-permute-done.5.refs_0_
  176.9 3.7 %collective-permute-done.6.refs_1_ = bf16[8,32,256]{2,1,0:T(8,128)(2,1)S(1)} collective-permute-done((bf16[8,32,256]{2,1,0:T(8,128)(2,1)S(1)}, bf16[8,32,256]{2,1,0:T(8,128)(2,1)S(1)}, u32[]{:S(2)}, u32[]{:S(2)}) %collective-permute-start.6) | collective-permute-done | bytes 131104 | tf_op jit(solution)/shard_map/ppermute | solution.py:329
  180.6 1.0 collective-permute-done.7.refs_2_
  181.6 0.0 copy-done.1
  181.6 1.6 place_averages.1
  (6 shorter events, 0.0 us)
Async XLA Ops:
  2.6 4.2 %collective-permute-start = (bf16[17,128,128]{2,1,0:T(8,128)(2,1)}, bf16[17,128,128]{2,1,0:T(8,128)(2,1)}, u32[]{:S(2)}, u32[]{:S(2)}) collective-permute-start(bf16[17,128,128]{2,1,0:T(8,128)(2,1)} %prepare.1.own_in), channel_id=1, source_target_pairs={{0,1},{1,0},{2,3},{3,2},{4,5},{5,4},{6,7},{7,6},{8,9},{9,8},{10,11... | collective-permute-start | bytes 1671176 | tf_op jit(solution)/shard_map/ppermute | solution.py:329
  16.1 59.4 %collective-permute-start.1 = (bf16[8,96,128]{2,1,0:T(8,128)(2,1)}, bf16[8,96,128]{2,1,0:T(8,128)(2,1)S(1)}, u32[]{:S(2)}, u32[]{:S(2)}) collective-permute-start(bf16[8,96,128]{2,1,0:T(8,128)(2,1)} %get-tuple-element.11), channel_id=1, source_target_pairs={{0,8},{8,16},{16,24},{24,32},{32,40},{40,48},{48,56},{56,64},{64,7... | collective-permute-start | bytes 589832 | tf_op jit(solution)/shard_map/ppermute | solution.py:329
  20.0 55.6 %collective-permute-start.4 = (bf16[8,96,128]{2,1,0:T(8,128)(2,1)}, bf16[8,96,128]{2,1,0:T(8,128)(2,1)S(1)}, u32[]{:S(2)}, u32[]{:S(2)}) collective-permute-start(bf16[8,96,128]{2,1,0:T(8,128)(2,1)} %get-tuple-element.14), channel_id=1, source_target_pairs={{0,248},{8,0},{16,8},{24,16},{32,24},{40,32},{48,40},{56,48},{64,5... | collective-permute-start | bytes 589832 | tf_op jit(solution)/shard_map/ppermute | solution.py:329
  63.4 10.9 %collective-permute-start.2 = (bf16[4,96,128]{2,1,0:T(8,128)(2,1)}, bf16[4,96,128]{2,1,0:T(8,128)(2,1)S(1)}, u32[]{:S(2)}, u32[]{:S(2)}) collective-permute-start(bf16[4,96,128]{2,1,0:T(8,128)(2,1)} %get-tuple-element.12), channel_id=1, source_target_pairs={{0,16},{8,24},{16,32},{24,40},{32,48},{40,56},{48,64},{56,72},{64,... | collective-permute-start | bytes 294920 | tf_op jit(solution)/shard_map/ppermute | solution.py:329
  65.4 10.2 %collective-permute-start.3 = (bf16[4,96,128]{2,1,0:T(8,128)(2,1)}, bf16[4,96,128]{2,1,0:T(8,128)(2,1)S(1)}, u32[]{:S(2)}, u32[]{:S(2)}) collective-permute-start(bf16[4,96,128]{2,1,0:T(8,128)(2,1)} %get-tuple-element.13), channel_id=1, source_target_pairs={{0,240},{8,248},{16,0},{24,8},{32,16},{40,24},{48,32},{56,40},{64,... | collective-permute-start | bytes 294920 | tf_op jit(solution)/shard_map/ppermute | solution.py:329
  75.6 0.9 copy-start
  76.5 47.2 %copy-start.4 = (bf16[2,128,256]{2,1,0:T(8,128)(2,1)S(1)}, bf16[2,128,256]{2,1,0:T(8,128)(2,1)}, u32[]{:S(2)}) copy-start(bf16[2,128,256]{2,1,0:T(8,128)(2,1)} %constant.31.clone.mix_cols_ref) | copy-start | bytes 393220
  77.3 46.5 %copy-start.2 = (bf16[2,256,512]{2,1,0:T(8,128)(2,1)S(1)}, bf16[2,256,512]{2,1,0:T(8,128)(2,1)}, u32[]{:S(2)}) copy-start(bf16[2,256,512]{2,1,0:T(8,128)(2,1)} %constant.30.clone.mix_rows_ref) | copy-start | bytes 1572868
  77.3 46.5 %copy-start.3 = (bf16[2,512,256]{2,1,0:T(8,128)(2,1)S(1)}, bf16[2,512,256]{2,1,0:T(8,128)(2,1)}, u32[]{:S(2)}) copy-start(bf16[2,512,256]{2,1,0:T(8,128)(2,1)} %constant.32.clone.last_rows_ref) | copy-start | bytes 1572868
  77.3 32.7 %all-to-all-start = ((bf16[8,96,128]{2,1,0:T(8,128)(2,1)}), bf16[8,96,128]{2,1,0:T(8,128)(2,1)S(1)}, u32[]{:S(2)}, u32[]{:S(2)}) async-start(bf16[8,96,128]{2,1,0:T(8,128)(2,1)} %collect.1), calls=%async_computation | async-start | bytes 393216 | tf_op jit(solution)/shard_map/all_to_all | solution.py:370
  127.1 54.5 %copy-start.1 = (s32[2]{0:T(128)S(1)}, s32[2]{0:T(128)}, u32[]{:S(2)}) copy-start(s32[2]{0:T(128)} %pad_add_fusion.place_ref) | copy-start | bytes 28
  167.1 9.8 %collective-permute-start.5 = (bf16[8,32,256]{2,1,0:T(8,128)(2,1)S(1)}, bf16[8,32,256]{2,1,0:T(8,128)(2,1)S(1)}, u32[]{:S(2)}, u32[]{:S(2)}) collective-permute-start(bf16[8,32,256]{2,1,0:T(8,128)(2,1)S(1)} %all_to_all.10.own_ref), channel_id=1, source_target_pairs={{0,248},{8,0},{16,8},{24,16},{32,24},{40,32},{48,40},{56,48},{64,5... | collective-permute-start | bytes 393224 | tf_op jit(solution)/shard_map/ppermute | solution.py:329
  171.5 9.1 %collective-permute-start.6 = (bf16[8,32,256]{2,1,0:T(8,128)(2,1)S(1)}, bf16[8,32,256]{2,1,0:T(8,128)(2,1)S(1)}, u32[]{:S(2)}, u32[]{:S(2)}) collective-permute-start(bf16[8,32,256]{2,1,0:T(8,128)(2,1)S(1)} %all_to_all.10.own_ref), channel_id=1, source_target_pairs={{0,240},{8,248},{16,0},{24,8},{32,16},{40,24},{48,32},{56,40},{64,... | collective-permute-start | bytes 393224 | tf_op jit(solution)/shard_map/ppermute | solution.py:329
  173.5 8.1 %collective-permute-start.7 = (bf16[8,32,256]{2,1,0:T(8,128)(2,1)S(1)}, bf16[8,32,256]{2,1,0:T(8,128)(2,1)S(1)}, u32[]{:S(2)}, u32[]{:S(2)}) collective-permute-start(bf16[8,32,256]{2,1,0:T(8,128)(2,1)S(1)} %all_to_all.10.own_ref), channel_id=1, source_target_pairs={{0,8},{8,16},{16,24},{24,32},{32,40},{40,48},{48,56},{56,64},{64,7... | collective-permute-start | bytes 393224 | tf_op jit(solution)/shard_map/ppermute | solution.py:329

commit v6 on v4

--- a/solution.py
+++ b/solution.py
@@ -358,29 +358,16 @@
     return added(lax.all_to_all(here, axis, 0, 0, axis_index_groups=strided(lax.axis_size(axis), NEAR)))
 
 
-def place_kernel(place_ref, own_ref, *refs):
-    out_ref = refs[-1]
-    n_class = out_ref.shape[0]
-    for ref, d in zip((own_ref, *refs[:-1]), (0, 1, 2, -1)):
-        first = (place_ref[1] + d + n_class) % NEAR
-        for i in range(own_ref.shape[0]):
-            out_ref[NEAR * i + first] = ref[i].astype(F32)
-
-
-def from_all(copies, axis, place):
+def neighbours(n, size):
+    return [[first + i for i in range(size)] for first in range(0, n, size)]
+
+
+def from_all(copies, axis):
     n = lax.axis_size(axis)
-    own = lax.all_to_all(copies, axis, 0, 0, axis_index_groups=strided(n, NEAR))
-    near = [shift(own, axis, -1), shift(own, axis, -2), shift(own, axis, 1)]
-    vmem = pl.BlockSpec(memory_space=pltpu.VMEM)
-    return pl.pallas_call(
-        place_kernel,
-        out_shape=jax.ShapeDtypeStruct((n, *copies.shape[1:]), F32),
-        in_specs=[pl.BlockSpec(memory_space=pltpu.SMEM)] + [vmem] * NEAR,
-        out_specs=vmem,
-        cost_estimate=pl.CostEstimate(flops=10**6, bytes_accessed=2 * 10**6, transcendentals=0),
-        compiler_params=pltpu.CompilerParams(vmem_limit_bytes=16 * 2**20),
-        name="place_averages",
-    )(place, own, *near)
+    far = lax.all_to_all(copies, axis, 0, 0, axis_index_groups=strided(n, NEAR))
+    far = jnp.broadcast_to(far, (NEAR, *far.shape))
+    every = lax.all_to_all(far, axis, 0, 0, axis_index_groups=neighbours(n, NEAR))
+    return jnp.swapaxes(every, 0, 1).reshape(n, *copies.shape[1:])
 
 
 def per_device(spectra, defocus, classes, poses, probs, counts, offsets, row_kernel, col_kernel):
@@ -397,7 +384,7 @@
     copies = refine_class(
         planes, jnp.asarray(mix_rows), jnp.asarray(mix_cols), jnp.asarray(last_rows), mine, n_class // NEAR
     )
-    return from_all(copies, "parts", place)
+    return from_all(copies, "parts").astype(F32)
 
 
 def solution(mesh):

time: 182 us -> 184 us (1.011)
  blocking collectives: 45.2 us -> 69 us
  waiting for transfers between devices: 50.1 us -> 38.7 us
  starting transfers between devices: 66.2 us -> 57.8 us
  Pallas kernels: 16 us -> 13.6 us
    all_to_all x1 -> x2, blocking collectives: 31.5 us -> 55.3 us  [the longest x1 35.5 us: from_all(): far = lax.all_to_all(copies, axis, 0, 0, axis_index_groups=strided(n, NEAR))]
    ppermute x7 -> x4, starting transfers between devices: 62.5 us -> 51.2 us  [shift(): return lax.ppermute(value, axis, [(i, (i + by) % n) for i in range(n)])]
    ppermute x7 -> x4, waiting for transfers between devices: 17.1 us -> 9 us  [shift(): return lax.ppermute(value, axis, [(i, (i + by) % n) for i in range(n)])]
    all_to_all x1, waiting for transfers between devices: 33 us -> 29.7 us  [sum_at_owner(): lax.all_to_all(here, axis, 0, 0, axis_index_groups=strided(lax.axis_size(...]
    all_to_all x1, starting transfers between devices: 3.73 us -> 6.57 us  [sum_at_owner(): lax.all_to_all(here, axis, 0, 0, axis_index_groups=strided(lax.axis_size(...]
  transfers between devices with their start and end apart: 8 -> 5, of which waited for: 6 -> 4; matrix products, arithmetic and copies ran while one was open for 1% -> 1% of each run, Pallas kernels for 0% -> 0%
where the time goes in v6:
time: 184 us; the launch traced here: 183 us
  blocking collectives  69 us (38%)
  starting transfers between devices  57.8 us (31%)
  waiting for transfers between devices  38.7 us (21%)
  Pallas kernels  13.6 us (7%)
    ppermute x4, starting transfers between devices, shift(): return lax.ppermute(value, axis, [(i, (i + by) % n) for i in range(n)])  51.2 us
    all_to_all x1, blocking collectives, from_all(): far = lax.all_to_all(copies, axis, 0, 0, axis_index_groups=strided(n, NEAR))  35.5 us
    all_to_all x1, waiting for transfers between devices, sum_at_owner(): lax.all_to_all(here, axis, 0, 0, axis_index_groups=strided(lax.axis_size(...  29.7 us
    all_to_all x1, blocking collectives, from_all(): lax.all_to_all(far, axis, 0, 0, axis_index_groups=neighbours(n, NEAR))  19.8 us
    all_gather x1, blocking collectives, per_device(): lax.all_gather(sum_at_owner(parts, 'parts'), ('sub', 'pair'), axis=0, til...  13.7 us
    ppermute x4, waiting for transfers between devices, shift(): return lax.ppermute(value, axis, [(i, (i + by) % n) for i in range(n)])  9 us
    pallas_call x1, Pallas kernels, insert_particles(): pl.pallas_call(particle_kernel, out_shape=[jax.ShapeDtypeStruct((n_class...  7.57 us
    all_to_all x1, starting transfers between devices, sum_at_owner(): lax.all_to_all(here, axis, 0, 0, axis_index_groups=strided(lax.axis_size(...  6.57 us
  transfers between devices with their start and end apart: 5, of which 4 were waited for; matrix products, arithmetic and copies ran while one was open for 1% of the time, Pallas kernels for 0%

profile of v6, /device:TPU:40, one launch (start us, length us, event | category | flops | bytes accessed | tf_op | source)
XLA Modules:
  0.0 183.3 jit_solution(4167719822006202009)
XLA Ops:
  0.7 1.9 %prepare.1.own_in = bf16[17,128,128]{2,1,0:T(8,128)(2,1)} custom-call(s32[1]{0:T(128)S(6)} %copy.16.counts_in, bf16[4,16]{1,0:T(4,128)(2,1)} %bitcast.14, bf16[1,16]{1,0:T(2,128)(2,1)} %bitcast.15, s32[4,16]{1,0:T(4,128)} %bitcast.12, s32[4,16]{1,0:T(4,128)} %bitcast.13, bf16[16,128,128]{2,1,0:T(8,128)(2,1)} %spec_in.1), custom_call_target="tpu_custom_call" | custom-call | flops 1000000 | bytes 2000000 | tf_op jit(solution)/shard_map/prepare/pallas_call | solution.py:88
  2.6 2.0 %collective-permute-start = (bf16[17,128,128]{2,1,0:T(8,128)(2,1)}, bf16[17,128,128]{2,1,0:T(8,128)(2,1)}, u32[]{:S(2)}, u32[]{:S(2)}) collective-permute-start(bf16[17,128,128]{2,1,0:T(8,128)(2,1)} %prepare.1.own_in), channel_id=1, source_target_pairs={{0,1},{1,0},{2,3},{3,2},{4,5},{5,4},{6,7},{7,6},{8,9},{9,8},{10,11... | collective-permute-start | bytes 1671176 | tf_op jit(solution)/shard_map/ppermute | solution.py:325
  4.5 0.6 pad_add_fusion.place_ref
  5.1 1.7 collective-permute-done.other_in
  6.8 7.6 %insert_particles.1 = (bf16[8,96,128]{2,1,0:T(8,128)(2,1)}, bf16[8,96,128]{2,1,0:T(8,128)(2,1)}, bf16[8,96,128]{2,1,0:T(8,128)(2,1)}, bf16[8,96,128]{2,1,0:T(8,128)(2,1)}) custom-call(s32[2]{0:T(128)} %pad_add_fusion.place_ref, s32[32]{0:T(128)} %offsets_in.1, bf16[32,64,64]{2,1,0:T(8,128)(2,1)} %rk_in.1, bf16[32,64,128]{2,1,0:T(8,128)(2,1)} %bitcast.16, ...), custom_call_target="tpu_custom_call" | custom-call | flops 5368709120 | bytes 1572864 | tf_op jit(solution)/shard_map/insert_particles/pallas_call | solution.py:208
  14.4 3.0 %collective-permute-start.1 = (bf16[8,96,128]{2,1,0:T(8,128)(2,1)}, bf16[8,96,128]{2,1,0:T(8,128)(2,1)S(1)}, u32[]{:S(2)}, u32[]{:S(2)}) collective-permute-start(bf16[8,96,128]{2,1,0:T(8,128)(2,1)} %get-tuple-element.10), channel_id=1, source_target_pairs={{0,8},{8,16},{16,24},{24,32},{32,40},{40,48},{48,56},{56,64},{64,7... | collective-permute-start | bytes 589832 | tf_op jit(solution)/shard_map/ppermute | solution.py:325
  17.3 8.7 %collective-permute-start.2 = (bf16[8,96,128]{2,1,0:T(8,128)(2,1)}, bf16[8,96,128]{2,1,0:T(8,128)(2,1)S(1)}, u32[]{:S(2)}, u32[]{:S(2)}) collective-permute-start(bf16[8,96,128]{2,1,0:T(8,128)(2,1)} %get-tuple-element.11), channel_id=1, source_target_pairs={{0,16},{8,24},{16,32},{24,40},{32,48},{40,56},{48,64},{56,72},{64,... | collective-permute-start | bytes 589832 | tf_op jit(solution)/shard_map/ppermute | solution.py:325
  26.0 37.6 %collective-permute-start.3 = (bf16[8,96,128]{2,1,0:T(8,128)(2,1)}, bf16[8,96,128]{2,1,0:T(8,128)(2,1)S(1)}, u32[]{:S(2)}, u32[]{:S(2)}) collective-permute-start(bf16[8,96,128]{2,1,0:T(8,128)(2,1)} %get-tuple-element.12), channel_id=1, source_target_pairs={{0,248},{8,0},{16,8},{24,16},{32,24},{40,32},{48,40},{56,48},{64,5... | collective-permute-start | bytes 589832 | tf_op jit(solution)/shard_map/ppermute | solution.py:325
  63.6 2.2 %collective-permute-done.1.b_ref = bf16[8,96,128]{2,1,0:T(8,128)(2,1)S(1)} collective-permute-done((bf16[8,96,128]{2,1,0:T(8,128)(2,1)}, bf16[8,96,128]{2,1,0:T(8,128)(2,1)S(1)}, u32[]{:S(2)}, u32[]{:S(2)}) %collective-permute-start.1) | collective-permute-done | bytes 196640 | tf_op jit(solution)/shard_map/ppermute | solution.py:325
  65.9 5.1 %collective-permute-done.2.c_ref = bf16[8,96,128]{2,1,0:T(8,128)(2,1)S(1)} collective-permute-done((bf16[8,96,128]{2,1,0:T(8,128)(2,1)}, bf16[8,96,128]{2,1,0:T(8,128)(2,1)S(1)}, u32[]{:S(2)}, u32[]{:S(2)}) %collective-permute-start.2) | collective-permute-done | bytes 196640 | tf_op jit(solution)/shard_map/ppermute | solution.py:325
  70.9 0.0 collective-permute-done.3.d_ref
  71.0 0.0 copy-start
  71.0 0.9 copy-done
  71.9 0.0 copy-start.3
  71.9 0.8 collect.1
  72.7 0.0 copy-start.1
  72.7 0.0 copy-start.2
  72.7 6.6 %all-to-all-start = ((bf16[8,96,128]{2,1,0:T(8,128)(2,1)}), bf16[8,96,128]{2,1,0:T(8,128)(2,1)S(1)}, u32[]{:S(2)}, u32[]{:S(2)}) async-start(bf16[8,96,128]{2,1,0:T(8,128)(2,1)} %collect.1), calls=%async_computation | async-start | bytes 393216 | tf_op jit(solution)/shard_map/all_to_all | solution.py:358
  79.2 0.8 dynamic-slice_bitcast_fusion.last_cols_ref
  80.0 29.7 %all-to-all-done = bf16[8,96,128]{2,1,0:T(8,128)(2,1)S(1)} async-done(((bf16[8,96,128]{2,1,0:T(8,128)(2,1)}), bf16[8,96,128]{2,1,0:T(8,128)(2,1)S(1)}, u32[]{:S(2)}, u32[]{:S(2)}) %all-to-all-start) | async-done | bytes 196640 | tf_op jit(solution)/shard_map/all_to_all | solution.py:358
  109.7 13.7 %all_gather.4.planes_ref = f32[8,96,128]{2,1,0:T(8,128)S(1)} all-gather(f32[1,96,128]{2,1,0:T(8,128)S(1)} %convert_add_fusion), channel_id=1, replica_groups=mesh['groups'=2,'parts'=32,'sub'=4,'pair'=2] {'sub','pair'}, dimensions={0}, use_global_device_ids=true | all-gather | bytes 442368 | tf_op jit(solution)/shard_map/all_gather | solution.py:381
  123.4 0.0 copy-done.3
  123.4 0.0 copy-done.1
  123.4 0.0 copy-done.2
  123.4 3.4 %refine_class.1 = bf16[8,32,256]{2,1,0:T(8,128)(2,1)S(1)} custom-call(f32[8,96,128]{2,1,0:T(8,128)S(1)} %all_gather.4.planes_ref, bf16[2,256,512]{2,1,0:T(8,128)(2,1)S(1)} %copy-done.1, bf16[2,128,256]{2,1,0:T(8,128)(2,1)S(1)} %copy-done.3, bf16[2,512,256]{2,1,0:T(8,128)(2,1)S(1)} %copy-done.2, bf16[2,64,128]{2,1,0:T(8,128)(2,1)S(1)} %dynamic-slice_bitcast_fusion.last_cols_ref), custom_call_target="tpu_custom_call" | custom-call | flops 2000000000 | bytes 3000000 | tf_op jit(solution)/shard_map/refine_class/pallas_call | solution.py:312
  126.8 35.5 %all_to_all.15 = bf16[8,32,256]{2,1,0:T(8,128)(2,1)S(1)} all-to-all(bf16[8,32,256]{2,1,0:T(8,128)(2,1)S(1)} %refine_class.1), channel_id=1, replica_groups={{0,32,64,96,128,160,192,224},{8,40,72,104,136,168,200,232},{16,48,80,11..., dimensions={0} | all-to-all | bytes 262144 | tf_op jit(solution)/shard_map/all_to_all | solution.py:367
  162.4 19.8 %all_to_all.16 = bf16[4,8,32,256]{3,2,1,0:T(8,128)(2,1)S(1)} all-to-all(bf16[4,8,32,256]{3,2,1,0:T(8,128)(2,1)S(1)} %broadcast_in_dim.7), channel_id=1, replica_groups={{0,8,16,24},{32,40,48,56},{64,72,80,88},{96,104,112,120},{128,136,144,1..., dimensions={0} | all-to-all | bytes 1048576 | tf_op jit(solution)/shard_map/all_to_all | solution.py:369
  182.2 1.1 copy_convert_fusion
  (2 shorter events, 0.1 us)
Async XLA Ops:
  2.6 4.2 %collective-permute-start = (bf16[17,128,128]{2,1,0:T(8,128)(2,1)}, bf16[17,128,128]{2,1,0:T(8,128)(2,1)}, u32[]{:S(2)}, u32[]{:S(2)}) collective-permute-start(bf16[17,128,128]{2,1,0:T(8,128)(2,1)} %prepare.1.own_in), channel_id=1, source_target_pairs={{0,1},{1,0},{2,3},{3,2},{4,5},{5,4},{6,7},{7,6},{8,9},{9,8},{10,11... | collective-permute-start | bytes 1671176 | tf_op jit(solution)/shard_map/ppermute | solution.py:325
  14.4 51.5 %collective-permute-start.1 = (bf16[8,96,128]{2,1,0:T(8,128)(2,1)}, bf16[8,96,128]{2,1,0:T(8,128)(2,1)S(1)}, u32[]{:S(2)}, u32[]{:S(2)}) collective-permute-start(bf16[8,96,128]{2,1,0:T(8,128)(2,1)} %get-tuple-element.10), channel_id=1, source_target_pairs={{0,8},{8,16},{16,24},{24,32},{32,40},{40,48},{48,56},{56,64},{64,7... | collective-permute-start | bytes 589832 | tf_op jit(solution)/shard_map/ppermute | solution.py:325
  17.3 53.6 %collective-permute-start.2 = (bf16[8,96,128]{2,1,0:T(8,128)(2,1)}, bf16[8,96,128]{2,1,0:T(8,128)(2,1)S(1)}, u32[]{:S(2)}, u32[]{:S(2)}) collective-permute-start(bf16[8,96,128]{2,1,0:T(8,128)(2,1)} %get-tuple-element.11), channel_id=1, source_target_pairs={{0,16},{8,24},{16,32},{24,40},{32,48},{40,56},{48,64},{56,72},{64,... | collective-permute-start | bytes 589832 | tf_op jit(solution)/shard_map/ppermute | solution.py:325
  26.0 44.9 %collective-permute-start.3 = (bf16[8,96,128]{2,1,0:T(8,128)(2,1)}, bf16[8,96,128]{2,1,0:T(8,128)(2,1)S(1)}, u32[]{:S(2)}, u32[]{:S(2)}) collective-permute-start(bf16[8,96,128]{2,1,0:T(8,128)(2,1)} %get-tuple-element.12), channel_id=1, source_target_pairs={{0,248},{8,0},{16,8},{24,16},{32,24},{40,32},{48,40},{56,48},{64,5... | collective-permute-start | bytes 589832 | tf_op jit(solution)/shard_map/ppermute | solution.py:325
  71.0 0.9 copy-start
  71.9 51.5 %copy-start.3 = (bf16[2,128,256]{2,1,0:T(8,128)(2,1)S(1)}, bf16[2,128,256]{2,1,0:T(8,128)(2,1)}, u32[]{:S(2)}) copy-start(bf16[2,128,256]{2,1,0:T(8,128)(2,1)} %constant.31.clone.mix_cols_ref) | copy-start | bytes 393220
  72.7 50.8 %copy-start.1 = (bf16[2,256,512]{2,1,0:T(8,128)(2,1)S(1)}, bf16[2,256,512]{2,1,0:T(8,128)(2,1)}, u32[]{:S(2)}) copy-start(bf16[2,256,512]{2,1,0:T(8,128)(2,1)} %constant.30.clone.mix_rows_ref) | copy-start | bytes 1572868
  72.7 50.8 %copy-start.2 = (bf16[2,512,256]{2,1,0:T(8,128)(2,1)S(1)}, bf16[2,512,256]{2,1,0:T(8,128)(2,1)}, u32[]{:S(2)}) copy-start(bf16[2,512,256]{2,1,0:T(8,128)(2,1)} %constant.32.clone.last_rows_ref) | copy-start | bytes 1572868
  72.7 37.0 %all-to-all-start = ((bf16[8,96,128]{2,1,0:T(8,128)(2,1)}), bf16[8,96,128]{2,1,0:T(8,128)(2,1)S(1)}, u32[]{:S(2)}, u32[]{:S(2)}) async-start(bf16[8,96,128]{2,1,0:T(8,128)(2,1)} %collect.1), calls=%async_computation | async-start | bytes 393216 | tf_op jit(solution)/shard_map/all_to_all | solution.py:358
